TPU v7x, 128 devices: a whole 4x4x4 slice. The times are simulated.
128 devices in a mesh: section: 4 (over z), dp: 16 (over y_lo, x, core), mp: 2 (over y_hi).
Axes of the slice: x: 4, y: 4 (y_hi: 2, y_lo: 2; y = y_hi * 2 + y_lo), z: 4, core: 2. Of those that a mesh axis runs over, the one named last changes fastest.
Arguments:
- tokens: bfloat16 [3, 64, 4096], P(None, ('dp', 'mp')), may hold values from -6 to 6
- member_ids: int32 [3, 64], replicated, may hold values from 0 to 3
- cotangent: bfloat16 [3, 64, 4096], P(None, ('dp', 'mp')), may hold values from -6 to 6
- w_gate: bfloat16 [4, 4096, 14336], P('section', None, ('dp', 'mp')), may hold values from -0.09375 to 0.09375
- w_up: bfloat16 [4, 4096, 14336], P('section', None, ('dp', 'mp')), may hold values from -0.09375 to 0.09375
- w_down: bfloat16 [4, 14336, 4096], P('section', ('dp', 'mp')), may hold values from -0.046875 to 0.046875
- in_scale: float32 [4, 4, 4096], P('section'), may hold values from 0.5 to 1.5
- mid_scale: float32 [4, 4, 14336], P('section', None, ('dp', 'mp')), may hold values from 0.5 to 1.5
- out_scale: float32 [4, 4, 4096], P('section'), may hold values from 0.5 to 1.5
- norm_gain: float32 [4, 4096], P('section'), may hold values from 0.5 to 1.5
Outputs:
- layer_outputs: bfloat16 [4, 3, 64, 4096], P('section', None, ('dp', 'mp'))
- section_in_grads: bfloat16 [4, 3, 64, 4096], P('section', None, ('dp', 'mp'))
- grad_gate: bfloat16 [4, 4096, 14336], P('section', None, ('dp', 'mp'))
- grad_up: bfloat16 [4, 4096, 14336], P('section', None, ('dp', 'mp'))
- grad_down: bfloat16 [4, 14336, 4096], P('section', ('dp', 'mp'))
- grad_in_scale: float32 [4, 4, 4096], P('section')
- grad_mid_scale: float32 [4, 4, 14336], P('section', None, ('dp', 'mp'))
- grad_out_scale: float32 [4, 4, 4096], P('section')
- grad_gain: float32 [4, 4096], P('section')
All inputs are finite; a program needn't handle non-finite values.
Results may differ from a plain program's by a relative error of at most 0.038.
Values may be sent and summed in bfloat16 or wider, within the bound.
A program may use at most 128 MiB of HBM per device.

v0:
```python
import jax
import jax.numpy as jnp
from jax import lax
from jax.sharding import PartitionSpec as P

EPS = 1e-05
HIGH = lax.Precision.HIGHEST


def cut_along(array, dim, devices):
    before, after = (array.shape[:dim], array.shape[dim + 1 :])
    return jnp.moveaxis(array.reshape(*before, devices, -1, *after), dim, 0)


def sent_and_summed(array, axis, dim):
    devices = lax.axis_size(axis)
    parts = lax.all_to_all(cut_along(array, dim, devices), axis, 0, 0, tiled=True)
    return jnp.sum(parts.astype(jnp.float32), axis=0)


def copy_for_each(array, axis):
    devices = lax.axis_size(axis)
    return lax.all_to_all(
        jnp.broadcast_to(array[None], (devices, *array.shape)), axis, 0, 0, tiled=True
    )


def joined_along(parts, dim):
    parts = jnp.moveaxis(parts, 0, dim)
    shape = parts.shape
    return parts.reshape(*shape[:dim], shape[dim] * shape[dim + 1], *shape[dim + 2 :])


def gathered_copies(array, axis, dim):
    parts = copy_for_each(array, axis)
    return joined_along(parts, dim)


def passed_along(block, axis, distance):
    devices = range(lax.axis_size(axis))
    route = [(i - distance, i) for i in devices if i - distance in devices]
    return lax.ppermute(block, axis, route)


def over_pieces(array, axis):
    parts = lax.all_gather(array, axis).astype(jnp.float32)
    return parts.sum(axis=0)


def member_table(onehot, table):
    return jnp.dot(onehot, table, precision=HIGH)


def member_sums(onehot, values):
    return jnp.dot(onehot.T, values, precision=HIGH)


def contract_rows(left, right):
    return lax.dot_general(
        left, right, (((0,), (0,)), ((), ())), preferred_element_type=jnp.float32
    )


def contract_cols(left, right):
    return lax.dot_general(
        left, right, (((1,), (1,)), ((), ())), preferred_element_type=jnp.float32
    )


def row_sums(term, rows):
    return sent_and_summed(
        term(jnp.int32(0), rows * lax.axis_size(("dp", "mp"))).astype(jnp.bfloat16), ("dp", "mp"), 0
    )


def store(buffer, slot, value, valid):
    previous = lax.dynamic_index_in_dim(buffer, slot, 0, keepdims=False)
    return lax.dynamic_update_index_in_dim(buffer, jnp.where(valid, value, previous), slot, 0)


def fetch(buffer, slot):
    return lax.dynamic_index_in_dim(buffer, slot, 0, keepdims=False)


def on_device(
    tokens, member_ids, cotangent, w_gate, w_up, w_down, in_scale, mid_scale, out_scale, norm_gain
):
    sections = lax.axis_size("section")
    section = lax.axis_index("section")
    micro = tokens.shape[0]
    rows = tokens.shape[1]
    width = tokens.shape[2]
    group = lax.axis_index("dp") * lax.axis_size("mp") + lax.axis_index("mp")
    gate_w = w_gate[0]
    up_w = w_up[0]
    down_w = w_down[0]
    in_tab = in_scale[0]
    mid_tab = mid_scale[0]
    out_tab = out_scale[0]
    gain = norm_gain[0]
    hidden_width = gate_w.shape[1]
    members = in_tab.shape[0]
    labels = jnp.arange(members, dtype=jnp.int32)
    full_hot = (member_ids[:, :, None] == labels[None, None, :]).astype(jnp.float32)
    total = full_hot.shape[1]
    row_hot = lax.dynamic_slice_in_dim(full_hot, group * rows, rows, 1)
    ticks = micro + sections - 1

    def forward_tick(tick, carry):
        keep_input, keep_scaled, keep_gate, keep_up, keep_down, forward_out, arriving = carry
        batch = tick - section
        valid = jnp.logical_and(batch >= 0, batch < micro)
        slot = jnp.clip(batch, 0, micro - 1)
        current = jnp.where(section == 0, fetch(tokens, slot), arriving)
        hot_rows = fetch(row_hot, slot)
        hot_full = fetch(full_hot, slot)
        x_float = current.astype(jnp.float32)
        inv_rms = lax.rsqrt(jnp.mean(x_float * x_float, axis=-1, keepdims=True) + EPS)
        normed = x_float * inv_rms
        scaled = (normed * gain * member_table(hot_rows, in_tab)).astype(jnp.bfloat16)
        whole_scaled = gathered_copies(scaled, ("dp", "mp"), 0)
        gate_pre = jnp.dot(whole_scaled, gate_w, preferred_element_type=jnp.float32)
        up_pre = jnp.dot(whole_scaled, up_w, preferred_element_type=jnp.float32)
        hidden = (jax.nn.silu(gate_pre) * up_pre * member_table(hot_full, mid_tab)).astype(
            jnp.bfloat16
        )

        def down_term(start, count):
            return jnp.dot(hidden, down_w, preferred_element_type=jnp.float32)

        down_out = row_sums(down_term, rows)
        x_next = (x_float + down_out * member_table(hot_rows, out_tab)).astype(jnp.bfloat16)
        keep_input = store(keep_input, slot, current, valid)
        keep_scaled = store(keep_scaled, slot, whole_scaled, valid)
        keep_gate = store(keep_gate, slot, gate_pre, valid)
        keep_up = store(keep_up, slot, up_pre, valid)
        keep_down = store(keep_down, slot, down_out, valid)
        forward_out = store(forward_out, slot, x_next, valid)
        arriving = passed_along(x_next, "section", 1)
        return (keep_input, keep_scaled, keep_gate, keep_up, keep_down, forward_out, arriving)

    start_fwd = (
        jnp.zeros((micro, rows, width), jnp.bfloat16),
        jnp.zeros((micro, total, width), jnp.bfloat16),
        jnp.zeros((micro, total, hidden_width), jnp.float32),
        jnp.zeros((micro, total, hidden_width), jnp.float32),
        jnp.zeros((micro, rows, width), jnp.float32),
        jnp.zeros((micro, rows, width), jnp.bfloat16),
        jnp.zeros((rows, width), jnp.bfloat16),
    )
    keep_input, keep_scaled, keep_gate, keep_up, keep_down, forward_out, unused = lax.fori_loop(
        0, ticks, forward_tick, start_fwd
    )

    def backward_tick(tick, carry):
        (
            acc_gate,
            acc_up,
            acc_down,
            acc_mid,
            acc_in,
            acc_out,
            acc_gain,
            input_grads,
            arriving_grad,
        ) = carry
        batch = tick - (sections - 1 - section)
        valid = jnp.logical_and(batch >= 0, batch < micro)
        slot = jnp.clip(batch, 0, micro - 1)
        incoming = jnp.where(section == sections - 1, fetch(cotangent, slot), arriving_grad)
        grad_y = jnp.where(valid, incoming.astype(jnp.float32), 0.0)
        hot_rows = fetch(row_hot, slot)
        hot_full = fetch(full_hot, slot)
        x_float = fetch(keep_input, slot).astype(jnp.float32)
        whole_scaled = fetch(keep_scaled, slot)
        gate_pre = fetch(keep_gate, slot)
        up_pre = fetch(keep_up, slot)
        down_out = fetch(keep_down, slot)
        grad_local_out = member_sums(hot_rows, grad_y * down_out)
        scaled_cot = (grad_y * member_table(hot_rows, out_tab)).astype(jnp.bfloat16)
        whole_cot = gathered_copies(scaled_cot, ("dp", "mp"), 0)
        mid_tok = member_table(hot_full, mid_tab)
        sigma = jax.nn.sigmoid(gate_pre)
        silu_gate = gate_pre * sigma
        product = silu_gate * up_pre
        hidden = (product * mid_tok).astype(jnp.bfloat16)
        grad_hidden = contract_cols(whole_cot, down_w)
        acc_down = acc_down + contract_rows(hidden, whole_cot)
        acc_mid = acc_mid + member_sums(hot_full, grad_hidden * product)
        grad_product = grad_hidden * mid_tok
        grad_gate_pre = (grad_product * up_pre * sigma * (1.0 + gate_pre * (1.0 - sigma))).astype(
            jnp.bfloat16
        )
        grad_up_pre = (grad_product * silu_gate).astype(jnp.bfloat16)
        acc_gate = acc_gate + contract_rows(whole_scaled, grad_gate_pre)
        acc_up = acc_up + contract_rows(whole_scaled, grad_up_pre)

        def input_term(start, count):
            first = contract_cols(grad_gate_pre, gate_w)
            return first + contract_cols(grad_up_pre, up_w)

        grad_scaled = row_sums(input_term, rows)
        inv_rms = lax.rsqrt(jnp.mean(x_float * x_float, axis=-1, keepdims=True) + EPS)
        normed = x_float * inv_rms
        grad_local_in = member_sums(hot_rows, grad_scaled * normed * gain)
        grad_w = grad_scaled * member_table(hot_rows, in_tab)
        grad_local_gain = jnp.sum(grad_w * normed, axis=0)
        acc_in = acc_in + grad_local_in
        acc_out = acc_out + grad_local_out
        acc_gain = acc_gain + grad_local_gain
        grad_normed = grad_w * gain
        grad_x = inv_rms * (
            grad_normed - normed * jnp.mean(grad_normed * normed, axis=-1, keepdims=True)
        )
        grad_input = (grad_y + grad_x).astype(jnp.bfloat16)
        input_grads = store(input_grads, slot, grad_input, valid)
        arriving_grad = passed_along(grad_input, "section", -1)
        return (
            acc_gate,
            acc_up,
            acc_down,
            acc_mid,
            acc_in,
            acc_out,
            acc_gain,
            input_grads,
            arriving_grad,
        )

    start_bwd = (
        jnp.zeros(gate_w.shape, jnp.float32),
        jnp.zeros(up_w.shape, jnp.float32),
        jnp.zeros(down_w.shape, jnp.float32),
        jnp.zeros(mid_tab.shape, jnp.float32),
        jnp.zeros(in_tab.shape, jnp.float32),
        jnp.zeros(out_tab.shape, jnp.float32),
        jnp.zeros(gain.shape, jnp.float32),
        jnp.zeros((micro, rows, width), jnp.bfloat16),
        jnp.zeros((rows, width), jnp.bfloat16),
    )
    acc_gate, acc_up, acc_down, acc_mid, acc_in, acc_out, acc_gain, input_grads, unused_grad = (
        lax.fori_loop(0, ticks, backward_tick, start_bwd)
    )
    acc_in, acc_out, acc_gain = (
        over_pieces(acc_in.astype(jnp.bfloat16), ("dp", "mp")).astype(jnp.float32),
        over_pieces(acc_out.astype(jnp.bfloat16), ("dp", "mp")).astype(jnp.float32),
        over_pieces(acc_gain.astype(jnp.bfloat16), ("dp", "mp")).astype(jnp.float32),
    )
    return (
        forward_out[None],
        input_grads[None],
        acc_gate.astype(jnp.bfloat16)[None],
        acc_up.astype(jnp.bfloat16)[None],
        acc_down.astype(jnp.bfloat16)[None],
        acc_in[None],
        acc_mid[None],
        acc_out[None],
        acc_gain[None],
    )


def solution(mesh):
    in_specs = (
        P(None, ("dp", "mp"), None),
        P(),
        P(None, ("dp", "mp"), None),
        P("section", None, ("dp", "mp")),
        P("section", None, ("dp", "mp")),
        P("section", ("dp", "mp"), None),
        P("section", None, None),
        P("section", None, ("dp", "mp")),
        P("section", None, None),
        P("section", None),
    )
    out_specs = (
        P("section", None, ("dp", "mp"), None),
        P("section", None, ("dp", "mp"), None),
        P("section", None, ("dp", "mp")),
        P("section", None, ("dp", "mp")),
        P("section", ("dp", "mp"), None),
        P("section", None, None),
        P("section", None, ("dp", "mp")),
        P("section", None, None),
        P("section", None),
    )
    return jax.shard_map(
        on_device, mesh=mesh, in_specs=in_specs, out_specs=out_specs, check_vma=False
    )
```

profile of v0, /device:TPU:1, one launch (start us, length us, event | category | flops | bytes accessed | tf_op | source)
XLA Modules:
  0.0 903.8 jit_solution(3891995836280234919)
XLA Ops:
  10.0 6.6 copy.27
  16.6 6.5 copy.28
  26.6 308.6 %while.58 = (s32[]{:T(128)}, bf16[3,2,4096]{2,1,0:T(2,128)(2,1)}, bf16[3,64,4096]{2,1,0:T(8,128)(2,1)S(1)}, f32[3,64,448]{2,1,0:T(8,128)S(1)}, f32[3,64,448]{2,1...) while((s32[]{:T(128)}, bf16[3,2,4096]{2,1,0:T(2,128)(2,1)}, ...), condition=%wide.region_3.4_spmd, body=%wide.region_0.3_spmd.sunk | while | flops 708235264 | bytes 53082108 | solution.py:151
  29.9 8.6 all-to-all-start
  42.1 7.6 all-to-all-done
  62.6 11.0 %all-to-all-done.1 = bf16[32,2,4096]{2,1,0:T(2,128)(2,1)S(1)} async-done(((bf16[32,2,4096]{2,1,0:T(2,128)(2,1)}), bf16[32,2,4096]{2,1,0:T(2,128)(2,1)S(1)}, u32[]{:S(2)}, u32[]{:S(2)}) %all-to-all-start.1) | async-done | bytes 524320 | tf_op jit(solution)/shard_map/while/body/eval_jaxpr/all_to_all | solution.py:17
  92.9 7.7 all-to-all-done
  113.5 11.0 %all-to-all-done.1 = bf16[32,2,4096]{2,1,0:T(2,128)(2,1)S(1)} async-done(((bf16[32,2,4096]{2,1,0:T(2,128)(2,1)}), bf16[32,2,4096]{2,1,0:T(2,128)(2,1)S(1)}, u32[]{:S(2)}, u32[]{:S(2)}) %all-to-all-start.1) | async-done | bytes 524320 | tf_op jit(solution)/shard_map/while/body/eval_jaxpr/all_to_all | solution.py:17
  143.7 7.7 all-to-all-done
  164.3 11.0 %all-to-all-done.1 = bf16[32,2,4096]{2,1,0:T(2,128)(2,1)S(1)} async-done(((bf16[32,2,4096]{2,1,0:T(2,128)(2,1)}), bf16[32,2,4096]{2,1,0:T(2,128)(2,1)S(1)}, u32[]{:S(2)}, u32[]{:S(2)}) %all-to-all-start.1) | async-done | bytes 524320 | tf_op jit(solution)/shard_map/while/body/eval_jaxpr/all_to_all | solution.py:17
  194.5 7.7 all-to-all-done
  215.1 11.0 %all-to-all-done.1 = bf16[32,2,4096]{2,1,0:T(2,128)(2,1)S(1)} async-done(((bf16[32,2,4096]{2,1,0:T(2,128)(2,1)}), bf16[32,2,4096]{2,1,0:T(2,128)(2,1)S(1)}, u32[]{:S(2)}, u32[]{:S(2)}) %all-to-all-start.1) | async-done | bytes 524320 | tf_op jit(solution)/shard_map/while/body/eval_jaxpr/all_to_all | solution.py:17
  245.3 7.7 all-to-all-done
  265.9 11.0 %all-to-all-done.1 = bf16[32,2,4096]{2,1,0:T(2,128)(2,1)S(1)} async-done(((bf16[32,2,4096]{2,1,0:T(2,128)(2,1)}), bf16[32,2,4096]{2,1,0:T(2,128)(2,1)S(1)}, u32[]{:S(2)}, u32[]{:S(2)}) %all-to-all-start.1) | async-done | bytes 524320 | tf_op jit(solution)/shard_map/while/body/eval_jaxpr/all_to_all | solution.py:17
  296.1 7.7 all-to-all-done
  316.7 11.0 %all-to-all-done.1 = bf16[32,2,4096]{2,1,0:T(2,128)(2,1)S(1)} async-done(((bf16[32,2,4096]{2,1,0:T(2,128)(2,1)}), bf16[32,2,4096]{2,1,0:T(2,128)(2,1)S(1)}, u32[]{:S(2)}, u32[]{:S(2)}) %all-to-all-start.1) | async-done | bytes 524320 | tf_op jit(solution)/shard_map/while/body/eval_jaxpr/all_to_all | solution.py:17
  335.3 388.6 %while.59 = (s32[]{:T(128)}, f32[4096,448]{0,1:T(8,128)}, f32[4096,448]{0,1:T(8,128)}, f32[448,4096]{1,0:T(8,128)}, f32[4,448]{1,0:T(4,128)}, /*index=5*/f32[4,4...) while((s32[]{:T(128)}, f32[4096,448]{0,1:T(8,128)}, ...), condition=%wide.region_9.10_spmd.clone, body=%wide.region_4.9_spmd.clone.sunk | while | flops 1426787840 | bytes 98941712 | solution.py:242
  347.0 7.7 all-to-all-done.2
  358.2 5.2 select_add_fusion.10
  395.2 6.6 all-to-all-start.2
  405.5 7.5 all-to-all-done.2
  416.5 7.4 select_add_fusion.10
  433.0 7.2 select_add_fusion.8
  441.4 7.3 select_add_fusion.9
  460.1 8.5 all-to-all-start.2
  472.3 7.5 all-to-all-done.2
  483.3 7.4 select_add_fusion.10
  499.8 7.2 select_add_fusion.8
  508.1 7.3 select_add_fusion.9
  526.8 8.5 all-to-all-start.2
  539.0 7.5 all-to-all-done.2
  550.0 7.4 select_add_fusion.10
  566.5 7.2 select_add_fusion.8
  574.9 7.3 select_add_fusion.9
  593.5 8.5 all-to-all-start.2
  605.8 7.5 all-to-all-done.2
  616.8 7.4 select_add_fusion.10
  633.3 7.2 select_add_fusion.8
  641.6 7.3 select_add_fusion.9
  660.3 8.5 all-to-all-start.2
  672.5 7.5 all-to-all-done.2
  683.5 7.4 select_add_fusion.10
  700.0 7.2 select_add_fusion.8
  708.4 7.3 select_add_fusion.9
  727.0 5.5 convert_bitcast_fusion.1
  732.4 66.3 %all-gather.2 = bf16[131072]{0:T(1024)(128)(2,1)S(1)} all-gather(bf16[4096]{0:T(1024)(128)(2,1)S(1)} %convert_element_type.177), channel_id=4, replica_groups=mesh['section'=4,'dp'=16,'mp'=2] {'dp','mp'}, dimensions={0}, use_global_device_ids=true | all-gather | bytes 270336 | tf_op jit(solution)/shard_map/all_gather | solution.py:46
  799.5 9.4 %convert_bitcast_fusion.2 = (bf16[1,4096,448]{1,2,0:T(8,128)(2,1)}, bf16[1,4096,448]{1,2,0:T(8,128)(2,1)}) fusion(f32[4096,448]{0,1:T(8,128)} %get-tuple-element.988, f32[4096,448]{0,1:T(8,128)} %get-tuple-element.987), kind=kLoop, calls=%fused_computation.113 | loop fusion | flops 3670016 | bytes 22020096 | tf_op jit(solution)/shard_map/broadcast_in_dim | solution.py:253
  813.0 81.6 %all-gather.10.cloned.1.call-done = bf16[32,4,4096]{2,1,0:T(4,128)(2,1)} async-done(((bf16[1,4,4096]{2,1,0:T(4,128)(2,1)}), bf16[32,4,4096]{2,1,0:T(4,128)(2,1)}) %all-gather.10.cloned.1.call-update) | async-done | bytes 1048592 | tf_op jit(solution)/shard_map/all_gather | solution.py:46
  (439 shorter events, 391.1 us)
Async XLA Ops:
  7.2 803.5 %all-gather.8.cloned.1.call-start = ((), (), s32[]{:S(2)}) async-start(), calls=%async_computation.4 | async-start | bytes 1081344 | tf_op jit(solution)/shard_map/all_gather | solution.py:46
  29.9 19.9 %all-to-all-start = ((bf16[32,2,4096]{2,1,0:T(2,128)(2,1)}), bf16[32,2,4096]{2,1,0:T(2,128)(2,1)S(1)}, u32[]{:S(2)}, u32[]{:S(2)}) async-start(bf16[32,2,4096]{2,1,0:T(2,128)(2,1)} %broadcast_in_dim.177), calls=%async_computation | async-start | bytes 1048576 | tf_op jit(solution)/shard_map/while/body/eval_jaxpr/all_to_all | solution.py:23
  57.8 15.7 %all-to-all-start.1 = ((bf16[32,2,4096]{2,1,0:T(2,128)(2,1)}), bf16[32,2,4096]{2,1,0:T(2,128)(2,1)S(1)}, u32[]{:S(2)}, u32[]{:S(2)}) async-start(bf16[32,2,4096]{2,1,0:T(2,128)(2,1)} %reshape.151), calls=%async_computation.1 | async-start | bytes 1048576 | tf_op jit(solution)/shard_map/while/body/eval_jaxpr/all_to_all | solution.py:17
  75.7 5.5 collective-permute-start
  84.5 16.1 %all-to-all-start = ((bf16[32,2,4096]{2,1,0:T(2,128)(2,1)}), bf16[32,2,4096]{2,1,0:T(2,128)(2,1)S(1)}, u32[]{:S(2)}, u32[]{:S(2)}) async-start(bf16[32,2,4096]{2,1,0:T(2,128)(2,1)} %broadcast_in_dim.177), calls=%async_computation | async-start | bytes 1048576 | tf_op jit(solution)/shard_map/while/body/eval_jaxpr/all_to_all | solution.py:23
  108.7 15.8 %all-to-all-start.1 = ((bf16[32,2,4096]{2,1,0:T(2,128)(2,1)}), bf16[32,2,4096]{2,1,0:T(2,128)(2,1)S(1)}, u32[]{:S(2)}, u32[]{:S(2)}) async-start(bf16[32,2,4096]{2,1,0:T(2,128)(2,1)} %reshape.151), calls=%async_computation.1 | async-start | bytes 1048576 | tf_op jit(solution)/shard_map/while/body/eval_jaxpr/all_to_all | solution.py:17
  126.6 5.5 collective-permute-start
  135.3 16.1 %all-to-all-start = ((bf16[32,2,4096]{2,1,0:T(2,128)(2,1)}), bf16[32,2,4096]{2,1,0:T(2,128)(2,1)S(1)}, u32[]{:S(2)}, u32[]{:S(2)}) async-start(bf16[32,2,4096]{2,1,0:T(2,128)(2,1)} %broadcast_in_dim.177), calls=%async_computation | async-start | bytes 1048576 | tf_op jit(solution)/shard_map/while/body/eval_jaxpr/all_to_all | solution.py:23
  159.5 15.8 %all-to-all-start.1 = ((bf16[32,2,4096]{2,1,0:T(2,128)(2,1)}), bf16[32,2,4096]{2,1,0:T(2,128)(2,1)S(1)}, u32[]{:S(2)}, u32[]{:S(2)}) async-start(bf16[32,2,4096]{2,1,0:T(2,128)(2,1)} %reshape.151), calls=%async_computation.1 | async-start | bytes 1048576 | tf_op jit(solution)/shard_map/while/body/eval_jaxpr/all_to_all | solution.py:17
  177.4 5.5 collective-permute-start
  186.1 16.1 %all-to-all-start = ((bf16[32,2,4096]{2,1,0:T(2,128)(2,1)}), bf16[32,2,4096]{2,1,0:T(2,128)(2,1)S(1)}, u32[]{:S(2)}, u32[]{:S(2)}) async-start(bf16[32,2,4096]{2,1,0:T(2,128)(2,1)} %broadcast_in_dim.177), calls=%async_computation | async-start | bytes 1048576 | tf_op jit(solution)/shard_map/while/body/eval_jaxpr/all_to_all | solution.py:23
  210.3 15.8 %all-to-all-start.1 = ((bf16[32,2,4096]{2,1,0:T(2,128)(2,1)}), bf16[32,2,4096]{2,1,0:T(2,128)(2,1)S(1)}, u32[]{:S(2)}, u32[]{:S(2)}) async-start(bf16[32,2,4096]{2,1,0:T(2,128)(2,1)} %reshape.151), calls=%async_computation.1 | async-start | bytes 1048576 | tf_op jit(solution)/shard_map/while/body/eval_jaxpr/all_to_all | solution.py:17
  228.2 5.5 collective-permute-start
  236.9 16.1 %all-to-all-start = ((bf16[32,2,4096]{2,1,0:T(2,128)(2,1)}), bf16[32,2,4096]{2,1,0:T(2,128)(2,1)S(1)}, u32[]{:S(2)}, u32[]{:S(2)}) async-start(bf16[32,2,4096]{2,1,0:T(2,128)(2,1)} %broadcast_in_dim.177), calls=%async_computation | async-start | bytes 1048576 | tf_op jit(solution)/shard_map/while/body/eval_jaxpr/all_to_all | solution.py:23
  261.1 15.8 %all-to-all-start.1 = ((bf16[32,2,4096]{2,1,0:T(2,128)(2,1)}), bf16[32,2,4096]{2,1,0:T(2,128)(2,1)S(1)}, u32[]{:S(2)}, u32[]{:S(2)}) async-start(bf16[32,2,4096]{2,1,0:T(2,128)(2,1)} %reshape.151), calls=%async_computation.1 | async-start | bytes 1048576 | tf_op jit(solution)/shard_map/while/body/eval_jaxpr/all_to_all | solution.py:17
  279.0 5.5 collective-permute-start
  287.7 16.1 %all-to-all-start = ((bf16[32,2,4096]{2,1,0:T(2,128)(2,1)}), bf16[32,2,4096]{2,1,0:T(2,128)(2,1)S(1)}, u32[]{:S(2)}, u32[]{:S(2)}) async-start(bf16[32,2,4096]{2,1,0:T(2,128)(2,1)} %broadcast_in_dim.177), calls=%async_computation | async-start | bytes 1048576 | tf_op jit(solution)/shard_map/while/body/eval_jaxpr/all_to_all | solution.py:23
  311.9 15.8 %all-to-all-start.1 = ((bf16[32,2,4096]{2,1,0:T(2,128)(2,1)}), bf16[32,2,4096]{2,1,0:T(2,128)(2,1)S(1)}, u32[]{:S(2)}, u32[]{:S(2)}) async-start(bf16[32,2,4096]{2,1,0:T(2,128)(2,1)} %reshape.151), calls=%async_computation.1 | async-start | bytes 1048576 | tf_op jit(solution)/shard_map/while/body/eval_jaxpr/all_to_all | solution.py:17
  329.8 5.5 collective-permute-start
  338.6 16.1 %all-to-all-start.2 = ((bf16[32,2,4096]{2,1,0:T(2,128)(2,1)}), bf16[32,2,4096]{2,1,0:T(2,128)(2,1)S(1)}, u32[]{:S(2)}, u32[]{:S(2)}) async-start(bf16[32,2,4096]{2,1,0:T(2,128)(2,1)} %broadcast_in_dim.180), calls=%async_computation.2 | async-start | bytes 1048576 | tf_op jit(solution)/shard_map/while/body/eval_jaxpr/all_to_all | solution.py:23
  368.0 15.8 %all-to-all-start.3 = ((bf16[32,2,4096]{2,1,0:T(2,128)(2,1)}), bf16[32,2,4096]{2,1,0:T(2,128)(2,1)S(1)}, u32[]{:S(2)}, u32[]{:S(2)}) async-start(bf16[32,2,4096]{2,1,0:T(2,128)(2,1)} %reshape.153), calls=%async_computation.3 | async-start | bytes 1048576 | tf_op jit(solution)/shard_map/while/body/eval_jaxpr/all_to_all | solution.py:17
  377.7 11.1 %copy-start.4 = (f32[4096]{0:T(1024)S(1)}, f32[4096]{0:T(1024)}, u32[]{:S(2)}) copy-start(f32[4096]{0:T(1024)} %get-tuple-element.1763) | copy-start | bytes 49156 | tf_op jit(solution)/shard_map/while
  387.5 4.6 collective-permute-start.1
  395.2 17.9 %all-to-all-start.2 = ((bf16[32,2,4096]{2,1,0:T(2,128)(2,1)}), bf16[32,2,4096]{2,1,0:T(2,128)(2,1)S(1)}, u32[]{:S(2)}, u32[]{:S(2)}) async-start(bf16[32,2,4096]{2,1,0:T(2,128)(2,1)} %broadcast_in_dim.180), calls=%async_computation.2 | async-start | bytes 1048576 | tf_op jit(solution)/shard_map/while/body/eval_jaxpr/all_to_all | solution.py:23
  428.6 20.0 %all-to-all-start.3 = ((bf16[32,2,4096]{2,1,0:T(2,128)(2,1)}), bf16[32,2,4096]{2,1,0:T(2,128)(2,1)S(1)}, u32[]{:S(2)}, u32[]{:S(2)}) async-start(bf16[32,2,4096]{2,1,0:T(2,128)(2,1)} %reshape.153), calls=%async_computation.3 | async-start | bytes 1048576 | tf_op jit(solution)/shard_map/while/body/eval_jaxpr/all_to_all | solution.py:17
  441.4 7.7 copy-start.8
  441.4 12.3 %copy-start.4 = (f32[4096]{0:T(1024)S(1)}, f32[4096]{0:T(1024)}, u32[]{:S(2)}) copy-start(f32[4096]{0:T(1024)} %get-tuple-element.1763) | copy-start | bytes 49156 | tf_op jit(solution)/shard_map/while
  452.3 4.6 collective-permute-start.1
  460.1 19.8 %all-to-all-start.2 = ((bf16[32,2,4096]{2,1,0:T(2,128)(2,1)}), bf16[32,2,4096]{2,1,0:T(2,128)(2,1)S(1)}, u32[]{:S(2)}, u32[]{:S(2)}) async-start(bf16[32,2,4096]{2,1,0:T(2,128)(2,1)} %broadcast_in_dim.180), calls=%async_computation.2 | async-start | bytes 1048576 | tf_op jit(solution)/shard_map/while/body/eval_jaxpr/all_to_all | solution.py:23
  495.4 20.0 %all-to-all-start.3 = ((bf16[32,2,4096]{2,1,0:T(2,128)(2,1)}), bf16[32,2,4096]{2,1,0:T(2,128)(2,1)S(1)}, u32[]{:S(2)}, u32[]{:S(2)}) async-start(bf16[32,2,4096]{2,1,0:T(2,128)(2,1)} %reshape.153), calls=%async_computation.3 | async-start | bytes 1048576 | tf_op jit(solution)/shard_map/while/body/eval_jaxpr/all_to_all | solution.py:17
  508.1 7.7 copy-start.8
  508.1 12.3 %copy-start.4 = (f32[4096]{0:T(1024)S(1)}, f32[4096]{0:T(1024)}, u32[]{:S(2)}) copy-start(f32[4096]{0:T(1024)} %get-tuple-element.1763) | copy-start | bytes 49156 | tf_op jit(solution)/shard_map/while
  519.1 4.6 collective-permute-start.1
  526.8 19.8 %all-to-all-start.2 = ((bf16[32,2,4096]{2,1,0:T(2,128)(2,1)}), bf16[32,2,4096]{2,1,0:T(2,128)(2,1)S(1)}, u32[]{:S(2)}, u32[]{:S(2)}) async-start(bf16[32,2,4096]{2,1,0:T(2,128)(2,1)} %broadcast_in_dim.180), calls=%async_computation.2 | async-start | bytes 1048576 | tf_op jit(solution)/shard_map/while/body/eval_jaxpr/all_to_all | solution.py:23
  562.1 20.0 %all-to-all-start.3 = ((bf16[32,2,4096]{2,1,0:T(2,128)(2,1)}), bf16[32,2,4096]{2,1,0:T(2,128)(2,1)S(1)}, u32[]{:S(2)}, u32[]{:S(2)}) async-start(bf16[32,2,4096]{2,1,0:T(2,128)(2,1)} %reshape.153), calls=%async_computation.3 | async-start | bytes 1048576 | tf_op jit(solution)/shard_map/while/body/eval_jaxpr/all_to_all | solution.py:17
  574.8 7.7 copy-start.8
  574.9 12.3 %copy-start.4 = (f32[4096]{0:T(1024)S(1)}, f32[4096]{0:T(1024)}, u32[]{:S(2)}) copy-start(f32[4096]{0:T(1024)} %get-tuple-element.1763) | copy-start | bytes 49156 | tf_op jit(solution)/shard_map/while
  585.8 4.6 collective-permute-start.1
  593.5 19.8 %all-to-all-start.2 = ((bf16[32,2,4096]{2,1,0:T(2,128)(2,1)}), bf16[32,2,4096]{2,1,0:T(2,128)(2,1)S(1)}, u32[]{:S(2)}, u32[]{:S(2)}) async-start(bf16[32,2,4096]{2,1,0:T(2,128)(2,1)} %broadcast_in_dim.180), calls=%async_computation.2 | async-start | bytes 1048576 | tf_op jit(solution)/shard_map/while/body/eval_jaxpr/all_to_all | solution.py:23
  628.9 20.0 %all-to-all-start.3 = ((bf16[32,2,4096]{2,1,0:T(2,128)(2,1)}), bf16[32,2,4096]{2,1,0:T(2,128)(2,1)S(1)}, u32[]{:S(2)}, u32[]{:S(2)}) async-start(bf16[32,2,4096]{2,1,0:T(2,128)(2,1)} %reshape.153), calls=%async_computation.3 | async-start | bytes 1048576 | tf_op jit(solution)/shard_map/while/body/eval_jaxpr/all_to_all | solution.py:17
  641.6 12.3 %copy-start.4 = (f32[4096]{0:T(1024)S(1)}, f32[4096]{0:T(1024)}, u32[]{:S(2)}) copy-start(f32[4096]{0:T(1024)} %get-tuple-element.1763) | copy-start | bytes 49156 | tf_op jit(solution)/shard_map/while
  652.6 4.6 collective-permute-start.1
  660.3 19.8 %all-to-all-start.2 = ((bf16[32,2,4096]{2,1,0:T(2,128)(2,1)}), bf16[32,2,4096]{2,1,0:T(2,128)(2,1)S(1)}, u32[]{:S(2)}, u32[]{:S(2)}) async-start(bf16[32,2,4096]{2,1,0:T(2,128)(2,1)} %broadcast_in_dim.180), calls=%async_computation.2 | async-start | bytes 1048576 | tf_op jit(solution)/shard_map/while/body/eval_jaxpr/all_to_all | solution.py:23
  695.6 20.0 %all-to-all-start.3 = ((bf16[32,2,4096]{2,1,0:T(2,128)(2,1)}), bf16[32,2,4096]{2,1,0:T(2,128)(2,1)S(1)}, u32[]{:S(2)}, u32[]{:S(2)}) async-start(bf16[32,2,4096]{2,1,0:T(2,128)(2,1)} %reshape.153), calls=%async_computation.3 | async-start | bytes 1048576 | tf_op jit(solution)/shard_map/while/body/eval_jaxpr/all_to_all | solution.py:17
  708.4 12.3 %copy-start.4 = (f32[4096]{0:T(1024)S(1)}, f32[4096]{0:T(1024)}, u32[]{:S(2)}) copy-start(f32[4096]{0:T(1024)} %get-tuple-element.1763) | copy-start | bytes 49156 | tf_op jit(solution)/shard_map/while
  719.3 4.6 collective-permute-start.1
  723.9 8.5 copy-start.7
  725.4 169.2 %all-gather.10.cloned.1.call-start = ((), (), s32[]{:S(2)}) async-start(), calls=%async_computation.5 | async-start | bytes 1081344 | tf_op jit(solution)/shard_map/all_gather | solution.py:46
  (52 other events, 280.4 us)
Sparse Core Ops, SparseCore 0:
  725.5 85.1 all-gather.7
  812.9 81.6 all-gather.9
where the time goes:
time: 915 us; the launch traced here: 904 us
  waiting for transfers between devices  262 us (29%)
  matrix products  259 us (28%)
  starting transfers between devices  162 us (18%)
  local copies, waits for them, and re-layouts  75.2 us (8%)
  blocking collectives  66.3 us (7%)
  other arithmetic  62.7 us (7%)
  between operations  14.2 us (2%)
    dot_general x18, matrix products, contract_rows(): lax.dot_general(left, right, (((0,), (0,)), ((), ())), preferred_element_...  123 us
    all_to_all x12, waiting for transfers between devices, copy_for_each(): lax.all_to_all(jnp.broadcast_to(array[None], (devices, *array.shape)), ax...  91.6 us
    all_gather x2, waiting for transfers between devices, over_pieces(): parts = lax.all_gather(array, axis).astype(jnp.float32)  83.4 us
    all_to_all x12, starting transfers between devices, copy_for_each(): lax.all_to_all(jnp.broadcast_to(array[None], (devices, *array.shape)), ax...  77.1 us
    all_to_all x12, waiting for transfers between devices, sent_and_summed(): lax.all_to_all(cut_along(array, dim, devices), axis, 0, 0, tiled=True)  67.8 us
    all_gather x1, blocking collectives, over_pieces(): parts = lax.all_gather(array, axis).astype(jnp.float32)  66.3 us
    all_to_all x12, starting transfers between devices, sent_and_summed(): lax.all_to_all(cut_along(array, dim, devices), axis, 0, 0, tiled=True)  52.7 us
    dot_general x36, matrix products, member_table(): return jnp.dot(onehot, table, precision=HIGH)  43.7 us
  transfers between devices with their start and end apart: 38, of which 27 were waited for; matrix products, arithmetic and copies ran while one was open for 18% of the time, Pallas kernels for 0%

commit v1 on v0

v1 whole, which is shorter than its diff:
```python
import functools

import jax
import jax.numpy as jnp
from jax import lax
from jax.experimental import pallas as pl
from jax.experimental.pallas import tpu as pltpu
from jax.sharding import PartitionSpec as P

EPS = 1e-05
F32 = jnp.float32
BF16 = jnp.bfloat16


def nt_dot(left, right):
    return lax.dot_general(left, right, (((1,), (1,)), ((), ())), preferred_element_type=F32)


def pick(table, ids, members):
    rows = ids.shape[0]
    value = jnp.broadcast_to(table[members - 1 : members], (rows, table.shape[1]))
    for m in range(members - 1):
        value = jnp.where(ids == m, table[m : m + 1], value)
    return value


def relay_kernel(
    dims,
    tok, cot, ids, wg_h, wu_h, wd_h, in_tab, gain, out_tab, mid_tab,
    out, hid, dg, du, sc, ct, gtab, gmid,
    wg, wu, wd, sel, t1, initr, rowf, xin, gin, xg, gg, gt_tab, inv, gpre, upre,
    psend, precv, pown, pf, rbuf, csend, cprecv, cown, crbuf, down, ob, ig,
    acc_in, acc_out, gtl, outs, outr, outp,
    wsem, isem, zs, zr, ags, agr, ds, dr, ps, pr, rs, rr, cps, cpr, cs, cr, osem,
):
    sections, chips, micro, rows, members = dims
    width = in_tab.shape[1]
    hidden = mid_tab.shape[1]
    half = width // 2
    bw = half // chips
    total = rows * 2 * chips
    s = lax.axis_index("section")
    dp = lax.axis_index("dp")
    mp = lax.axis_index("mp")
    mps = lax.axis_size("mp")
    core = lax.rem(dp, 2)
    other = 1 - core
    q = (dp // 2) * mps + mp
    block = core * chips + q
    last = sections - 1
    partner = {"dp": (dp // 2) * 2 + other, "mp": mp}
    above = {"section": jnp.minimum(s + 1, last)}
    below = {"section": jnp.maximum(s - 1, 0)}

    def chip(j):
        to = lax.rem(q + j, chips)
        return to, {"dp": (to // mps) * 2 + core, "mp": lax.rem(to, mps)}

    def remote(src, dst, send, recv, device):
        return pltpu.make_async_remote_copy(
            src_ref=src, dst_ref=dst, send_sem=send, recv_sem=recv,
            device_id=device, device_id_type=pl.DeviceIdType.MESH,
        )

    def cols(index, size):
        return pl.ds(pl.multiple_of(index * size, size), size)

    weights = [
        pltpu.make_async_copy(h, v, wsem.at[i])
        for i, (h, v) in enumerate(((wg_h, wg), (wu_h, wu), (wd_h, wd)))
    ]
    for copy in weights:
        copy.start()

    barrier = pltpu.get_barrier_semaphore()
    for j in range(1, chips):
        pl.semaphore_signal(barrier, inc=1, device_id=chip(j)[1], device_id_type=pl.DeviceIdType.MESH)
    pl.semaphore_signal(barrier, inc=1, device_id=partner, device_id_type=pl.DeviceIdType.MESH)

    @pl.when(s < last)
    def _():
        pl.semaphore_signal(barrier, inc=1, device_id=above, device_id_type=pl.DeviceIdType.MESH)

    @pl.when(s > 0)
    def _():
        pl.semaphore_signal(barrier, inc=1, device_id=below, device_id_type=pl.DeviceIdType.MESH)

    @pl.when(s == 0)
    def _():
        sel[...] = tok[...]

    @pl.when(s > 0)
    def _():
        sel[...] = cot[...]

    gt_tab[...] = in_tab[...] * gain[...]
    acc_in[...] = jnp.zeros_like(acc_in)
    acc_out[...] = jnp.zeros_like(acc_out)
    gmid[...] = jnp.zeros_like(gmid)
    gtl[...] = jnp.zeros_like(gtl)
    pl.semaphore_wait(barrier, chips + (s < last).astype(jnp.int32) + (s > 0).astype(jnp.int32))

    mine = pl.ds(core * micro, micro)
    first = remote(sel.at[:, :, cols(other, half)], t1.at[mine], isem.at[0], isem.at[1], partner)
    first.start()
    t1[mine] = sel[:, :, cols(core, half)]
    first.wait_recv()
    for j in range(1, chips):
        to, device = chip(j)
        remote(t1.at[:, :, cols(to, bw)], initr.at[q], isem.at[2], isem.at[3], device).start()
    initr[q] = t1[:, :, cols(q, bw)]
    others = initr.at[pl.ds(0, chips - 1)]
    second = remote(others, others, isem.at[2], isem.at[3], partner)
    second.wait_recv()
    for k in range(micro):
        for i in range(chips):
            for c in range(2):
                at = (i * 2 + c) * rows
                rowf[at : at + rows, :] = initr[i, c * micro + k].astype(F32)

        @pl.when(s == 0)
        def _():
            xin[k] = rowf[...].astype(BF16)

        @pl.when(s == last)
        def _():
            gin[k] = rowf[...].astype(BF16)

    for copy in weights:
        copy.wait()

    my_cols = cols(block, bw)
    core_cols = cols(core, half)
    r15 = lambda ph, k: rbuf.at[ph, k, pl.ds(0, chips - 1)]

    def spread(ph, k, src, dst):
        dst[k, :, my_cols] = src[k]
        for j in range(1, chips):
            remote(src.at[k], dst.at[k, :, my_cols], ags.at[ph, k], agr.at[ph, k], chip(j)[1]).start()

    def gather_rest(ph, k, dst):
        remote(r15(ph, k), r15(ph, k), ags.at[ph, k], agr.at[ph, k], partner).wait_recv()
        part = dst.at[k, :, core_cols]
        copy = remote(part, part, ds.at[ph, k], dr.at[ph, k], partner)
        copy.start()
        copy.wait_recv()

    def reduce_out(ph, k, term):
        step = min(512, half)
        each = step // bw
        for n in range(half // step):
            value = term(pl.ds(pl.multiple_of(other * half + n * step, step), step))
            for e in range(each):
                psend[ph, k, n * each + e] = value[:, e * bw : (e + 1) * bw].astype(BF16)
        copy = remote(psend.at[ph, k], precv.at[ph, k], ps.at[ph, k], pr.at[ph, k], partner)
        copy.start()
        for n in range(half // step):
            value = term(pl.ds(pl.multiple_of(core * half + n * step, step), step))
            for e in range(each):
                pf[n * each + e] = value[:, e * bw : (e + 1) * bw]
        copy.wait_recv()
        for n in range(chips):
            pown[ph, k, n] = (pf[n] + precv[ph, k, n].astype(F32)).astype(BF16)
        for j in range(1, chips):
            to, device = chip(j)
            remote(pown.at[ph, k, to], rbuf.at[ph, k, q], rs.at[ph, k], rr.at[ph, k], device).start()
        rbuf[ph, k, q] = pown[ph, k, q]

    def reduced(ph, k):
        remote(r15(ph, k), r15(ph, k), rs.at[ph, k], rr.at[ph, k], partner).wait_recv()
        value = rbuf[ph, k, 0].astype(F32)
        for n in range(1, chips):
            value = value + rbuf[ph, k, n].astype(F32)
        return value

    chunk = min(512, width)
    pieces = [(at, min(256, hidden - at)) for at in range(0, hidden, 256)]

    def token_rows(k):
        return pl.ds(pl.multiple_of(k * total, total), total)

    def fwd_arrive(k):
        @pl.when(s > 0)
        def _():
            remote(xin.at[k], xin.at[k], zs.at[0, k], zr.at[0, k], above).wait_recv()

        spread(0, k, xin, xg)

    def fwd_compute(k):
        gather_rest(0, k, xg)
        here = token_rows(k)
        id_col = ids[k]
        squares = jnp.zeros((total, 128), F32)
        for n in range(width // 128):
            x = xg[k, :, n * 128 : (n + 1) * 128].astype(F32)
            squares = squares + x * x
        scale = lax.rsqrt(jnp.sum(squares, axis=-1, keepdims=True) * (1.0 / width) + EPS)
        inv[k] = scale

        def scale_chunk(n, carry):
            at = cols(n, chunk)
            x = xg[k, :, at].astype(F32)
            sc[here, at] = (x * scale * pick(gt_tab[:, at], id_col, members)).astype(BF16)
            return carry

        lax.fori_loop(0, width // chunk, scale_chunk, 0)
        for at, size in pieces:
            hs = slice(at, at + size)
            gate = nt_dot(wg[hs, :], sc[here, :]).T
            up = nt_dot(wu[hs, :], sc[here, :]).T
            gpre[k, :, hs] = gate
            upre[k, :, hs] = up
            product = gate / (1.0 + jnp.exp(-gate)) * up
            hid[here, hs] = (product * pick(mid_tab[:, hs], id_col, members)).astype(BF16)
        h = hid[here, :]
        reduce_out(0, k, lambda at: jnp.dot(h, wd[:, at], preferred_element_type=F32))

    def fwd_finish(k):
        value = reduced(0, k)
        down[k] = value
        x = xg[k, :, my_cols].astype(F32)
        ob[k] = (x + value * pick(out_tab[:, my_cols], ids[k], members)).astype(BF16)

        @pl.when(s < last)
        def _():
            remote(ob.at[k], xin.at[k], zs.at[0, k], zr.at[0, k], above).start()

    def bwd_arrive(k):
        @pl.when(s < last)
        def _():
            remote(gin.at[k], gin.at[k], zs.at[1, k], zr.at[1, k], below).wait_recv()

        spread(1, k, gin, gg)

    def bwd_compute(k):
        gather_rest(1, k, gg)
        here = token_rows(k)
        id_col = ids[k]

        def cot_chunk(n, carry):
            at = cols(n, chunk)
            g = gg[k, :, at].astype(F32)
            ct[here, at] = (g * pick(out_tab[:, at], id_col, members)).astype(BF16)
            return carry

        lax.fori_loop(0, width // chunk, cot_chunk, 0)
        dots = jnp.zeros((total, 1), F32)
        for at, size in pieces:
            hs = slice(at, at + size)
            grad_hidden = nt_dot(wd[hs, :], ct[here, :]).T
            gate = gpre[k, :, hs]
            up = upre[k, :, hs]
            sig = 1.0 / (1.0 + jnp.exp(-gate))
            silu = gate * sig
            mids = grad_hidden * (silu * up)
            for m in range(members):
                gmid[m : m + 1, hs] += jnp.sum(jnp.where(id_col == m, mids, 0.0), axis=0, keepdims=True)
            grad_product = grad_hidden * pick(mid_tab[:, hs], id_col, members)
            grad_gate = (grad_product * up * sig * (1.0 + gate * (1.0 - sig))).astype(BF16)
            grad_up = (grad_product * silu).astype(BF16)
            dg[here, hs] = grad_gate
            du[here, hs] = grad_up
            dots = dots + jnp.sum(
                grad_gate.astype(F32) * gate + grad_up.astype(F32) * up, axis=-1, keepdims=True
            )
        csend[k] = jnp.broadcast_to(dots, (total, 128)).T[0:8, :]
        ccopy = remote(csend.at[k], cprecv.at[k], cps.at[k], cpr.at[k], partner)
        ccopy.start()
        grad_gates = dg[here, :]
        grad_ups = du[here, :]

        def term(at):
            return jnp.dot(grad_gates, wg[:, at], preferred_element_type=F32) + jnp.dot(
                grad_ups, wu[:, at], preferred_element_type=F32
            )

        reduce_out(1, k, term)
        ccopy.wait_recv()
        cown[k] = csend[k] + cprecv[k]
        for j in range(1, chips):
            remote(cown.at[k], crbuf.at[k, q], cs.at[k], cr.at[k], chip(j)[1]).start()
        crbuf[k, q] = cown[k]

    def bwd_finish(k):
        id_col = ids[k]
        g = gin[k].astype(F32)
        grad_scaled = reduced(1, k)
        c15 = crbuf.at[k, pl.ds(0, chips - 1)]
        remote(c15, c15, cs.at[k], cr.at[k], partner).wait_recv()
        dots = crbuf[k, 0]
        for n in range(1, chips):
            dots = dots + crbuf[k, n]
        mean = dots.T[:, 0:1] * (1.0 / width)
        scale = inv[k]
        normed = xg[k, :, my_cols].astype(F32) * scale
        outs_here = g * down[k]
        ins_here = grad_scaled * normed
        for m in range(members):
            mask = id_col == m
            acc_out[m : m + 1, :] += jnp.sum(jnp.where(mask, outs_here, 0.0), axis=0, keepdims=True)
            acc_in[m : m + 1, :] += jnp.sum(jnp.where(mask, ins_here, 0.0), axis=0, keepdims=True)
        grad_normed = grad_scaled * pick(gt_tab[:, my_cols], id_col, members)
        ig[k] = (g + scale * (grad_normed - normed * mean)).astype(BF16)

        @pl.when(s > 0)
        def _():
            remote(ig.at[k], gin.at[k], zs.at[1, k], zr.at[1, k], below).start()

    def run(arrive, compute, finish):
        def tick(t, carry):
            @pl.when(t < micro)
            def _():
                arrive(t)

            @pl.when(jnp.logical_and(t >= 1, t < micro + 1))
            def _():
                compute(t - 1)

            @pl.when(t >= 2)
            def _():
                finish(t - 2)

            return carry

        lax.fori_loop(0, micro + 2, tick, 0)

    run(fwd_arrive, fwd_compute, fwd_finish)
    run(bwd_arrive, bwd_compute, bwd_finish)

    tables = acc_in[...]
    gtl[0:members, :] = tables * gain[:, my_cols]
    gtl[members : 2 * members, :] = acc_out[...]
    gtl[2 * members : 2 * members + 1, :] = jnp.sum(tables * in_tab[:, my_cols], axis=0, keepdims=True)
    gtab[:, my_cols] = gtl[...]
    for j in range(1, chips):
        remote(gtl, gtab.at[:, my_cols], osem.at[0], osem.at[1], chip(j)[1]).start()

    for kind, src in ((0, ob), (1, ig)):
        for k in range(micro):
            rowf[...] = src[k].astype(F32)
            for i in range(chips):
                for c in range(2):
                    at = (i * 2 + c) * rows
                    outs[i, (c * 2 + kind) * micro + k] = rowf[at : at + rows, :].astype(BF16)
    for j in range(1, chips):
        to, device = chip(j)
        remote(outs.at[to], outr.at[:, :, cols(q, bw)], osem.at[2], osem.at[3], device).start()
    outr[:, :, cols(q, bw)] = outs[q]

    most = gtab.at[:, pl.ds(0, (chips - 1) * bw)]
    remote(most, most, osem.at[0], osem.at[1], partner).wait_recv()
    table_part = gtab.at[:, core_cols]
    tables_on = remote(table_part, table_part, osem.at[4], osem.at[5], partner)
    tables_on.start()
    most_outs = outs.at[pl.ds(0, chips - 1)]
    remote(most_outs, most_outs, osem.at[2], osem.at[3], partner).wait_recv()
    rows_on = remote(outr.at[pl.ds(other * 2 * micro, 2 * micro)], outp, osem.at[6], osem.at[7], partner)
    rows_on.start()
    out[:, :, core_cols] = outr[pl.ds(core * 2 * micro, 2 * micro)]

    first.wait_send()
    second.wait_send()
    for ph in range(2):
        for k in range(micro):
            remote(r15(ph, k), r15(ph, k), ags.at[ph, k], agr.at[ph, k], partner).wait_send()
            remote(r15(ph, k), r15(ph, k), rs.at[ph, k], rr.at[ph, k], partner).wait_send()
            part = xg.at[k, :, core_cols]
            remote(part, part, ds.at[ph, k], dr.at[ph, k], partner).wait_send()
            remote(psend.at[ph, k], precv.at[ph, k], ps.at[ph, k], pr.at[ph, k], partner).wait_send()
    for k in range(micro):
        remote(csend.at[k], cprecv.at[k], cps.at[k], cpr.at[k], partner).wait_send()
        c15 = crbuf.at[k, pl.ds(0, chips - 1)]
        remote(c15, c15, cs.at[k], cr.at[k], partner).wait_send()

        @pl.when(s < last)
        def _():
            remote(ob.at[k], xin.at[k], zs.at[0, k], zr.at[0, k], above).wait_send()

        @pl.when(s > 0)
        def _():
            remote(ig.at[k], gin.at[k], zs.at[1, k], zr.at[1, k], below).wait_send()

    remote(most, most, osem.at[0], osem.at[1], partner).wait_send()
    remote(most_outs, most_outs, osem.at[2], osem.at[3], partner).wait_send()
    tables_on.wait()
    rows_on.wait()
    out[:, :, cols(other, half)] = outp[...]


def on_device(
    tokens, member_ids, cotangent, w_gate, w_up, w_down, in_scale, mid_scale, out_scale, norm_gain
):
    sections = lax.axis_size("section")
    mps = lax.axis_size("mp")
    places = lax.axis_size("dp") // 2
    chips = places * mps
    micro, rows, width = tokens.shape
    total = member_ids.shape[1]
    members = in_scale.shape[1]
    hidden = w_gate.shape[2]
    half = width // 2
    bw = half // chips
    ids = member_ids.reshape(micro, places, 2, mps, rows).transpose(0, 1, 3, 2, 4)
    ids = ids.reshape(micro, total, 1)
    gate_t = w_gate[0].T
    up_t = w_up[0].T
    down_w = w_down[0]
    all_tokens = micro * total
    vmem = pl.BlockSpec(memory_space=pltpu.VMEM)
    hbm = pl.BlockSpec(memory_space=pl.ANY)
    dma = pltpu.SemaphoreType.DMA

    def buf(*shape, dtype=BF16):
        return pltpu.VMEM(shape, dtype)

    dims = (sections, chips, micro, rows, members)
    outs = (
        jax.ShapeDtypeStruct((2 * micro, rows, width), BF16),
        jax.ShapeDtypeStruct((all_tokens, hidden), BF16),
        jax.ShapeDtypeStruct((all_tokens, hidden), BF16),
        jax.ShapeDtypeStruct((all_tokens, hidden), BF16),
        jax.ShapeDtypeStruct((all_tokens, width), BF16),
        jax.ShapeDtypeStruct((all_tokens, width), BF16),
        jax.ShapeDtypeStruct((16, width), F32),
        jax.ShapeDtypeStruct((members, hidden), F32),
    )
    out, hid, dg, du, sc, ct, gtab, gmid = pl.pallas_call(
        functools.partial(relay_kernel, dims),
        name="relay",
        out_shape=outs,
        in_specs=[vmem, vmem, vmem, hbm, hbm, hbm, vmem, vmem, vmem, vmem],
        out_specs=[vmem] * len(outs),
        scratch_shapes=[
            buf(hidden, width), buf(hidden, width), buf(hidden, width),
            buf(micro, rows, width),
            buf(2 * micro, rows, half),
            buf(chips, 2 * micro, rows, bw),
            buf(total, bw, dtype=F32),
            buf(micro, total, bw), buf(micro, total, bw),
            buf(micro, total, width), buf(micro, total, width),
            buf(members, width, dtype=F32),
            buf(micro, total, 1, dtype=F32),
            buf(micro, total, hidden, dtype=F32), buf(micro, total, hidden, dtype=F32),
            buf(2, micro, chips, total, bw), buf(2, micro, chips, total, bw),
            buf(2, micro, chips, total, bw),
            buf(chips, total, bw, dtype=F32),
            buf(2, micro, chips, total, bw),
            buf(micro, 8, total, dtype=F32), buf(micro, 8, total, dtype=F32),
            buf(micro, 8, total, dtype=F32), buf(micro, chips, 8, total, dtype=F32),
            buf(micro, total, bw, dtype=F32),
            buf(micro, total, bw), buf(micro, total, bw),
            buf(members, bw, dtype=F32), buf(members, bw, dtype=F32),
            buf(16, bw, dtype=F32),
            buf(chips, 4 * micro, rows, bw),
            buf(4 * micro, rows, half),
            buf(2 * micro, rows, half),
            dma((3,)), dma((4,)),
            dma((2, micro)), dma((2, micro)), dma((2, micro)), dma((2, micro)),
            dma((2, micro)), dma((2, micro)), dma((2, micro)), dma((2, micro)),
            dma((2, micro)), dma((2, micro)),
            dma((micro,)), dma((micro,)), dma((micro,)), dma((micro,)),
            dma((8,)),
        ],
        compiler_params=pltpu.CompilerParams(
            collective_id=0, has_side_effects=True, vmem_limit_bytes=56 * 1024 * 1024
        ),
    )(
        tokens, cotangent, ids, gate_t, up_t, down_w,
        in_scale[0], norm_gain, out_scale[0], mid_scale[0],
    )

    def weight_grad(left, right):
        return lax.dot_general(
            left, right, (((0,), (0,)), ((), ())), preferred_element_type=F32
        ).astype(BF16)

    return (
        out[:micro][None],
        out[micro:][None],
        weight_grad(dg, sc).T[None],
        weight_grad(du, sc).T[None],
        weight_grad(hid, ct)[None],
        gtab[:members][None],
        gmid[None],
        gtab[members : 2 * members][None],
        gtab[2 * members : 2 * members + 1],
    )


def solution(mesh):
    in_specs = (
        P(None, ("dp", "mp"), None),
        P(),
        P(None, ("dp", "mp"), None),
        P("section", None, ("dp", "mp")),
        P("section", None, ("dp", "mp")),
        P("section", ("dp", "mp"), None),
        P("section", None, None),
        P("section", None, ("dp", "mp")),
        P("section", None, None),
        P("section", None),
    )
    out_specs = (
        P("section", None, ("dp", "mp"), None),
        P("section", None, ("dp", "mp"), None),
        P("section", None, ("dp", "mp")),
        P("section", None, ("dp", "mp")),
        P("section", ("dp", "mp"), None),
        P("section", None, None),
        P("section", None, ("dp", "mp")),
        P("section", None, None),
        P("section", None),
    )
    return jax.shard_map(
        on_device, mesh=mesh, in_specs=in_specs, out_specs=out_specs, check_vma=False
    )
```

time: 915 us -> 255 us (0.28); the launches traced: 904 us -> 255 us
  waiting for transfers between devices: 262 us -> 0 us
  matrix products: 259 us -> 10.4 us
  Pallas kernels: 0 us -> 236 us
  starting transfers between devices: 162 us -> 0 us
  local copies, waits for them, and re-layouts: 75.2 us -> 7.04 us
  blocking collectives: 66.3 us -> 0 us
  other arithmetic: 62.7 us -> 0 us
  between operations: 14.2 us -> 0.7 us
    dot_general x108 -> x3, matrix products: 259 us -> 10.4 us  [weight_grad(): lax.dot_general(left, right, (((0,), (0,)), ((), ())), preferred_element_...]
    pallas_call x0 -> x1, Pallas kernels: none -> 236 us  [on_device(): pl.pallas_call(functools.partial(relay_kernel, dims), name='relay', out_s...]
    all_to_all x24 -> x0, waiting for transfers between devices: 159 us -> none  [the longest x12 91.6 us: copy_for_each(): lax.all_to_all(jnp.broadcast_to(array[None], (devices, *array.shape)), ax...]
    all_to_all x24 -> x0, starting transfers between devices: 130 us -> none  [the longest x12 77.1 us: copy_for_each(): lax.all_to_all(jnp.broadcast_to(array[None], (devices, *array.shape)), ax...]
    all_gather x2 -> x0, waiting for transfers between devices: 83.4 us -> none  [over_pieces(): parts = lax.all_gather(array, axis).astype(jnp.float32)]
    all_gather x1 -> x0, blocking collectives: 66.3 us -> none  [over_pieces(): parts = lax.all_gather(array, axis).astype(jnp.float32)]
    ppermute x12 -> x0, starting transfers between devices: 32.2 us -> none  [passed_along(): return lax.ppermute(block, axis, route)]
    reduce_sum x27 -> x0, other arithmetic: 20.8 us -> none  [the longest x3 5.24 us: over_pieces(): return parts.sum(axis=0)]
  transfers between devices with their start and end apart: 38 -> 0, of which waited for: 27 -> 0; matrix products, arithmetic and copies ran while one was open for 18% -> 0% of each run, Pallas kernels for 0% -> 0%
where the time goes in v1:
time: 255 us
  Pallas kernels  236 us (93%)
  matrix products  10.4 us (4%)
  local copies, waits for them, and re-layouts  7.04 us (3%)
    pallas_call x1, Pallas kernels, on_device(): pl.pallas_call(functools.partial(relay_kernel, dims), name='relay', out_s...  236 us
    dot_general x3, matrix products, weight_grad(): lax.dot_general(left, right, (((0,), (0,)), ((), ())), preferred_element_...  10.4 us

profile of v1, /device:TPU:1, one launch (start us, length us, event | category | flops | bytes accessed | tf_op | source)
XLA Modules:
  0.0 254.6 jit_solution(1905813671795591859)
XLA Ops:
  0.6 0.8 reshape.24
  1.5 0.8 reshape.26.ids
  2.2 236.4 %relay.1 = (bf16[6,2,4096]{2,1,0:T(2,128)(2,1)}, bf16[192,448]{1,0:T(8,128)(2,1)}, bf16[192,448]{1,0:T(8,128)(2,1)}, bf16[192,448]{1,0:T(8,128)(2,1)}, bf16[192,...) custom-call(bf16[3,2,4096]{2,1,0:T(2,128)(2,1)} %tok.1, ...), custom_call_target="tpu_custom_call" | custom-call | tf_op jit(solution)/shard_map/relay/pallas_call | solution.py:427
  238.7 0.0 copy-start
  238.7 0.0 copy-start.2
  238.7 1.7 slice_bitcast_fusion.2
  240.4 1.5 slice.19
  241.9 1.7 slice_bitcast_fusion
  243.5 4.4 %fusion = bf16[1,4096,448]{1,2,0:T(8,128)(2,1)} fusion(bf16[192,4096]{1,0:T(8,128)(2,1)} %get-tuple-element.18, bf16[192,448]{1,0:T(8,128)(2,1)} %get-tuple-element.19), kind=kOutput, calls=%fused_computation.3 | convolution fusion | flops 706478080 | bytes 5414912 | tf_op jit(solution)/shard_map/dot_general | solution.py:473
  247.9 0.0 copy-done
  247.9 0.0 copy-done.2
  247.9 0.0 copy-start.1
  247.9 0.0 copy-start.3
  248.0 3.0 %fusion.1 = bf16[1,4096,448]{1,2,0:T(8,128)(2,1)} fusion(bf16[192,4096]{1,0:T(8,128)(2,1)S(1)} %copy-done, bf16[192,448]{1,0:T(8,128)(2,1)S(1)} %copy-done.2), kind=kOutput, calls=%fused_computation.4 | convolution fusion | flops 706478080 | bytes 5414912 | tf_op jit(solution)/shard_map/dot_general | solution.py:473
  251.0 0.0 copy-done.1
  251.0 0.0 copy-done.3
  251.0 0.0 copy-start.4
  251.0 3.0 %fusion.2 = bf16[1,448,4096]{2,1,0:T(8,128)(2,1)} fusion(bf16[192,448]{1,0:T(8,128)(2,1)S(1)} %copy-done.3, bf16[192,4096]{1,0:T(8,128)(2,1)S(1)} %copy-done.1), kind=kOutput, calls=%fused_computation.5 | convolution fusion | flops 706478080 | bytes 5414912 | tf_op jit(solution)/shard_map/dot_general | solution.py:473
  254.0 0.0 copy-done.4
  254.0 0.6 copy.23
  (1 shorter events, 0.0 us)
Async XLA Ops:
  238.7 9.3 %copy-start = (bf16[192,4096]{1,0:T(8,128)(2,1)S(1)}, bf16[192,4096]{1,0:T(8,128)(2,1)}, u32[]{:S(2)}) copy-start(bf16[192,4096]{1,0:T(8,128)(2,1)} %get-tuple-element.18) | copy-start | bytes 4718596
  238.7 9.3 %copy-start.2 = (bf16[192,448]{1,0:T(8,128)(2,1)S(1)}, bf16[192,448]{1,0:T(8,128)(2,1)}, u32[]{:S(2)}) copy-start(bf16[192,448]{1,0:T(8,128)(2,1)} %get-tuple-element.20) | copy-start | bytes 516100
  247.9 3.0 %copy-start.1 = (bf16[192,4096]{1,0:T(8,128)(2,1)S(1)}, bf16[192,4096]{1,0:T(8,128)(2,1)}, u32[]{:S(2)}) copy-start(bf16[192,4096]{1,0:T(8,128)(2,1)} %get-tuple-element.22) | copy-start | bytes 4718596
  247.9 3.0 %copy-start.3 = (bf16[192,448]{1,0:T(8,128)(2,1)S(1)}, bf16[192,448]{1,0:T(8,128)(2,1)}, u32[]{:S(2)}) copy-start(bf16[192,448]{1,0:T(8,128)(2,1)} %get-tuple-element.21) | copy-start | bytes 516100
  251.0 3.0 %copy-start.4 = (f32[4,448]{1,0:T(4,128)S(1)}, f32[4,448]{1,0:T(4,128)}, u32[]{:S(2)}) copy-start(f32[4,448]{1,0:T(4,128)} %get-tuple-element.24) | copy-start | bytes 21508

commit v2 on v1

v2 whole, which is shorter than its diff:
```python
import functools

import jax
import jax.numpy as jnp
from jax import lax
from jax.experimental import pallas as pl
from jax.experimental.pallas import tpu as pltpu
from jax.sharding import PartitionSpec as P

EPS = 1e-05
F32 = jnp.float32
BF16 = jnp.bfloat16


def nt_dot(left, right):
    return lax.dot_general(left, right, (((1,), (1,)), ((), ())), preferred_element_type=F32)


def pick(table, ids, members):
    rows = ids.shape[0]
    value = jnp.broadcast_to(table[members - 1 : members], (rows, table.shape[1]))
    for m in range(members - 1):
        value = jnp.where(ids == m, table[m : m + 1], value)
    return value


def relay_kernel(
    dims,
    tok, cot, ids, wg_h, wu_h, wd_h, in_tab, gain, out_tab, mid_tab,
    out_x, out_g, hid_t, dg_t, du_t, sc_h, ct_h, g_in, g_out, g_gain, gmid,
    hid, dg, du, sc, ct,
    wg, wu, wd, rg, t1, initr, rowf, xin, gin, xg, gg, gt_tab, idc, inv, pacc, phid, gpre, upre,
    psend, precv, pown, pf, rbuf, csend, cprecv, cown, crbuf, down, ob, ig,
    acc_in, acc_out, gtl, gtab, outs, outr, outp,
    wsem, hsem, isem, xs, xr, xds, xdr, zs, zr, ags, agr, ds, dr, ps, pr, rs, rr, cps, cpr, cs, cr, osem,
):
    sections, places, mps, micro, rows, members = dims
    chips = places * mps
    across = places // 2
    width = in_tab.shape[1]
    hidden = mid_tab.shape[1]
    half = width // 2
    bw = half // chips
    total = rows * 2 * chips
    s = lax.axis_index("section")
    dp = lax.axis_index("dp")
    mp = lax.axis_index("mp")
    core = lax.rem(dp, 2)
    other = 1 - core
    place = dp // 2
    along_x = lax.rem(place, across)
    y_low = place // across
    along_y = mp * 2 + y_low
    q = place * mps + mp
    block = core * chips + q
    last = sections - 1
    partner = {"dp": place * 2 + other, "mp": mp}
    up_s = jnp.minimum(s + 1, last)
    down_s = jnp.maximum(s - 1, 0)
    above = {"section": up_s}
    below = {"section": down_s}

    def hops(d):
        return min(d[0], across - d[0]) + min(d[1], 2 * mps - d[1])

    offsets = [(dx, dy) for dx in range(across) for dy in range(2 * mps) if dx or dy]
    offsets.sort(key=lambda d: -hops(d))
    reach = hops(offsets[0]) // 2

    def chip(dx, dy):
        x = lax.rem(along_x + dx, across)
        y = lax.rem(along_y + dy, 2 * mps)
        at = lax.rem(y, 2) * across + x
        return at * mps + y // 2, {"dp": at * 2 + core, "mp": y // 2}

    peers = [chip(*d) for d in offsets]
    far = [p for p, d in zip(peers, offsets) if hops(d) > reach]
    near = [p for p, d in zip(peers, offsets) if hops(d) <= reach]
    groups = [
        [p for p, d in zip(peers, offsets) if d[1] % 2 == 1],
        [p for p, d in zip(peers, offsets) if d[1] % 2 == 0],
    ]

    def remote(src, dst, send, recv, device):
        return pltpu.make_async_remote_copy(
            src_ref=src, dst_ref=dst, send_sem=send, recv_sem=recv,
            device_id=device, device_id_type=pl.DeviceIdType.MESH,
        )

    def cols(index, size):
        return pl.ds(pl.multiple_of(index * size, size), size)

    weights = [
        pltpu.make_async_copy(h, v, wsem.at[i])
        for i, (h, v) in enumerate(((wg_h, wg), (wu_h, wu), (wd_h, wd)))
    ]
    for copy in weights:
        copy.start()

    barrier = pltpu.get_barrier_semaphore()
    for _, device in peers:
        pl.semaphore_signal(barrier, inc=1, device_id=device, device_id_type=pl.DeviceIdType.MESH)
    pl.semaphore_signal(barrier, inc=1, device_id=partner, device_id_type=pl.DeviceIdType.MESH)

    @pl.when(s < last)
    def _():
        for device in [above] + [{**d, **above} for _, d in far]:
            pl.semaphore_signal(barrier, inc=1, device_id=device, device_id_type=pl.DeviceIdType.MESH)

    @pl.when(s > 0)
    def _():
        for device in [below] + [{**d, **below} for _, d in far]:
            pl.semaphore_signal(barrier, inc=1, device_id=device, device_id_type=pl.DeviceIdType.MESH)

    gt_tab[...] = in_tab[...] * gain[...]
    acc_in[...] = jnp.zeros_like(acc_in)
    acc_out[...] = jnp.zeros_like(acc_out)
    gmid[...] = jnp.zeros_like(gmid)
    gtl[...] = jnp.zeros_like(gtl)
    i = lax.broadcasted_iota(jnp.int32, (total, total), 0)
    j = lax.broadcasted_iota(jnp.int32, (total, total), 1)
    i_mp = (i // (2 * rows)) % mps
    i_core = (i // rows) % 2
    source = (((i // (2 * rows * mps)) * 2 + i_core) * mps + i_mp) * rows + i % rows
    for k in range(micro):
        picked = jnp.where(source == j, jnp.broadcast_to(ids[k : k + 1, :], (total, total)), 0)
        idc[k] = jnp.sum(picked.astype(F32), axis=1, keepdims=True).astype(jnp.int32)
    links = (s < last).astype(jnp.int32) + (s > 0).astype(jnp.int32)
    pl.semaphore_wait(barrier, chips + (1 + len(far)) * links)

    my_cols = cols(block, bw)
    core_cols = cols(core, half)
    r15 = lambda ph, k: rbuf.at[ph, k, pl.ds(0, chips - 1)]

    def spread(ph, k, src, dst, targets):
        for _, device in targets:
            remote(src.at[k], dst.at[k, :, my_cols], ags.at[ph, k], agr.at[ph, k], device).start()
        dst[k, :, my_cols] = src[k]

    def hand_on(ph, k, src, dst, gathered, section):
        remote(src.at[k], dst.at[k], zs.at[ph, k], zr.at[ph, k], section).start()
        for _, device in far:
            remote(
                src.at[k], gathered.at[k, :, my_cols], zs.at[ph, k], agr.at[ph, k], {**device, **section}
            ).start()

    row_part = lambda k, c: rg.at[pl.ds(c * chips, chips), k]

    @pl.when(s == 0)
    def _():
        for k in range(micro):
            for _, device in peers:
                remote(tok.at[k], rg.at[block, k], xs.at[k], xr.at[k], device).start()
            rg[block, k] = tok[k]

    def forward_rows(k):
        most_rows = rg.at[pl.ds(0, chips - 1), k]
        remote(most_rows, most_rows, xs.at[k], xr.at[k], partner).wait_recv()
        remote(row_part(k, core), row_part(k, core), xds.at[k], xdr.at[k], partner).start()

    def place_rows(k):
        remote(row_part(k, other), row_part(k, other), xds.at[k], xdr.at[k], partner).wait_recv()
        for c in range(2):
            for n in range(chips):
                at = (n * 2 + c) * rows
                xg[k, at : at + rows, :] = rg[c * chips + n, k]

    mine = pl.ds(core * micro, micro)
    first = remote(cot.at[:, :, cols(other, half)], t1.at[mine], isem.at[0], isem.at[1], partner)
    others = initr.at[pl.ds(0, chips - 1)]
    second = remote(others, others, isem.at[2], isem.at[3], partner)

    @pl.when(s == last)
    def _():
        first.start()
        t1[mine] = cot[:, :, cols(core, half)]
        first.wait_recv()
        for to, device in peers:
            remote(t1.at[:, :, cols(to, bw)], initr.at[q], isem.at[2], isem.at[3], device).start()
        initr[q] = t1[:, :, cols(q, bw)]
        second.wait_recv()
        for k in range(micro):
            for n in range(chips):
                for c in range(2):
                    at = (n * 2 + c) * rows
                    rowf[at : at + rows, :] = initr[n, c * micro + k].astype(F32)
            gin[k] = rowf[...].astype(BF16)
            spread(1, k, gin, gg, peers)

    for copy in weights:
        copy.wait()

    chunk = min(512, half)
    pieces = [(at, min(256, hidden - at)) for at in range(0, hidden, 256)]

    def part_cols(c, n, size):
        return pl.ds(pl.multiple_of(c * half + n * size, size), size)

    def gathered(ph, k):
        remote(r15(ph, k), r15(ph, k), ags.at[ph, k], agr.at[ph, k], partner).wait_recv()

    def reduce_out(ph, k, term, between=None):
        step = min(512, half // 2)
        each = step // bw
        halves = half // 2 // step
        copies = []
        for piece in range(2):
            low = 1 - y_low if piece == 0 else y_low
            with jax.named_scope("down_other"):
                for n in range(halves):
                    at = other * half + low * (half // 2) + n * step
                    value = term(pl.ds(pl.multiple_of(at, step), step))
                    for e in range(each):
                        to = low * (chips // 2) + n * each + e
                        psend[ph, k, to] = value[:, e * bw : (e + 1) * bw].astype(BF16)
            at = pl.ds(low * (chips // 2), chips // 2)
            copy = remote(
                psend.at[ph, k, at], precv.at[ph, k, at], ps.at[ph, k, piece], pr.at[ph, k, piece], partner
            )
            copy.start()
            copies.append(copy)
        with jax.named_scope("down_own"):
            for n in range(half // step):
                value = term(pl.ds(pl.multiple_of(core * half + n * step, step), step))
                for e in range(each):
                    pf[n * each + e] = value[:, e * bw : (e + 1) * bw]
        if between is not None:
            between()
        for piece in range(2):
            low = 1 - y_low if piece == 0 else y_low
            with jax.named_scope("partner_wait"):
                copies[piece].wait_recv()
            with jax.named_scope("combine"):
                for n in range(chips // 2):
                    at = low * (chips // 2) + n
                    pown[ph, k, at] = (pf[at] + precv[ph, k, at].astype(F32)).astype(BF16)
                for to, device in groups[piece]:
                    remote(pown.at[ph, k, to], rbuf.at[ph, k, q], rs.at[ph, k], rr.at[ph, k], device).start()
        rbuf[ph, k, q] = pown[ph, k, q]

    def reduced(ph, k):
        with jax.named_scope("reduce_wait"):
            remote(r15(ph, k), r15(ph, k), rs.at[ph, k], rr.at[ph, k], partner).wait_recv()
        value = rbuf[ph, k, 0].astype(F32)
        for n in range(1, chips):
            value = value + rbuf[ph, k, n].astype(F32)
        return value

    def token_rows(k):
        return pl.ds(pl.multiple_of(k * total, total), total)

    def fwd_arrive(k):
        with jax.named_scope("x_wait"):
            @pl.when(s > 0)
            def _():
                remote(xin.at[k], xin.at[k], zs.at[0, k], zr.at[0, k], above).wait_recv()
                spread(0, k, xin, xg, near)

            @pl.when(jnp.logical_and(s == 0, k == 0))
            def _():
                forward_rows(k)

    def fwd_compute(k):
        here = token_rows(k)
        id_col = idc[k]

        def scaled_half(c, squares):
            def step(n, carry):
                at = part_cols(c, n, chunk)
                x = xg[k, :, at].astype(F32)
                sc[here, at] = (x * pick(gt_tab[:, at], id_col, members)).astype(BF16)
                x2 = x * x
                for e in range(chunk // 128):
                    carry = carry + x2[:, e * 128 : (e + 1) * 128]
                return carry

            return lax.fori_loop(0, half // chunk, step, squares)

        part = xg.at[k, :, core_cols]
        copy = remote(part, part, ds.at[0, k], dr.at[0, k], partner)
        with jax.named_scope("gather_wait"):
            @pl.when(s > 0)
            def _():
                gathered(0, k)
                copy.start()

            @pl.when(s == 0)
            def _():
                place_rows(k)

        with jax.named_scope("gateup_own"):
            squares = scaled_half(core, jnp.zeros((total, 128), F32))
            at = core_cols
            for h, size in pieces:
                hs = slice(h, h + size)
                pacc[0, hs, :] = nt_dot(wg[hs, at], sc[here, at])
                pacc[1, hs, :] = nt_dot(wu[hs, at], sc[here, at])
        with jax.named_scope("forward_wait"):
            @pl.when(s > 0)
            def _():
                copy.wait_recv()

            @pl.when(jnp.logical_and(s == 0, k < micro - 1))
            def _():
                forward_rows(jnp.minimum(k + 1, micro - 1))

        with jax.named_scope("gateup_other"):
            squares = scaled_half(other, squares)
            scale = lax.rsqrt(jnp.sum(squares, axis=-1, keepdims=True) * (1.0 / width) + EPS)
            inv[k] = scale
            at = cols(other, half)
            for h, size in pieces:
                hs = slice(h, h + size)
                gate = (pacc[0, hs, :] + nt_dot(wg[hs, at], sc[here, at])).T * scale
                up = (pacc[1, hs, :] + nt_dot(wu[hs, at], sc[here, at])).T * scale
                gpre[k, :, hs] = gate
                upre[k, :, hs] = up
                product = gate / (1.0 + jnp.exp(-gate)) * up
                hid[here, hs] = (product * pick(mid_tab[:, hs], id_col, members)).astype(BF16)
        h = hid[here, :]
        reduce_out(0, k, lambda at: jnp.dot(h, wd[:, at], preferred_element_type=F32))

    def fwd_finish(k):
        value = reduced(0, k)
        with jax.named_scope("fwd_finish"):
            x = xg[k, :, my_cols].astype(F32)
            ob[k] = (x + value * pick(out_tab[:, my_cols], idc[k], members)).astype(BF16)

            @pl.when(s < last)
            def _():
                hand_on(0, k, ob, xin, xg, above)

            down[k] = value

    def bwd_arrive(k):
        with jax.named_scope("g_wait"):
            remote(gin.at[k], gin.at[k], zs.at[1, k], zr.at[1, k], below).wait_recv()
        with jax.named_scope("g_spread"):
            spread(1, k, gin, gg, near)

    def bwd_hidden(k):
        here = token_rows(k)
        id_col = idc[k]

        def cot_half(c):
            def step(n, carry):
                at = part_cols(c, n, chunk)
                g = gg[k, :, at].astype(F32)
                ct[here, at] = (g * pick(out_tab[:, at], id_col, members)).astype(BF16)
                return carry

            lax.fori_loop(0, half // chunk, step, 0)

        with jax.named_scope("g_gather_wait"):
            gathered(1, k)
            part = gg.at[k, :, core_cols]
            copy = remote(part, part, ds.at[1, k], dr.at[1, k], partner)
            copy.start()
        with jax.named_scope("hidden_own"):
            cot_half(core)
            at = core_cols
            for h, size in pieces:
                hs = slice(h, h + size)
                phid[k, hs, :] = nt_dot(wd[hs, at], ct[here, at])
        with jax.named_scope("g_forward_wait"):
            copy.wait_recv()
        with jax.named_scope("hidden_other"):
            cot_half(other)
            at = cols(other, half)
            for h, size in pieces:
                hs = slice(h, h + size)
                phid[k, hs, :] += nt_dot(wd[hs, at], ct[here, at])

    def bwd_compute(k):
        here = token_rows(k)
        id_col = idc[k]
        with jax.named_scope("grads"):
            scale = inv[k]
            dots = jnp.zeros((total, 1), F32)
            grad_gates = []
            grad_ups = []
            for h, size in pieces:
                hs = slice(h, h + size)
                grad_hidden = phid[k, hs, :].T
                gate = gpre[k, :, hs]
                up = upre[k, :, hs]
                sig = 1.0 / (1.0 + jnp.exp(-gate))
                silu = gate * sig
                mids = grad_hidden * (silu * up)
                for m in range(members):
                    gmid[m : m + 1, hs] += jnp.sum(jnp.where(id_col == m, mids, 0.0), axis=0, keepdims=True)
                grad_product = grad_hidden * pick(mid_tab[:, hs], id_col, members)
                grad_gate = grad_product * up * sig * (1.0 + gate * (1.0 - sig))
                grad_up = grad_product * silu
                dg[here, hs] = (grad_gate * scale).astype(BF16)
                du[here, hs] = (grad_up * scale).astype(BF16)
                grad_gate = grad_gate.astype(BF16)
                grad_up = grad_up.astype(BF16)
                grad_gates.append(grad_gate)
                grad_ups.append(grad_up)
                dots = dots + jnp.sum(
                    grad_gate.astype(F32) * gate + grad_up.astype(F32) * up, axis=-1, keepdims=True
                )
            csend[k] = jnp.broadcast_to(dots, (total, 128)).T[0:8, :]
            ccopy = remote(csend.at[k], cprecv.at[k], cps.at[k], cpr.at[k], partner)
            ccopy.start()
            grad_gates = jnp.concatenate(grad_gates, axis=1)
            grad_ups = jnp.concatenate(grad_ups, axis=1)

        def term(at):
            return jnp.dot(grad_gates, wg[:, at], preferred_element_type=F32) + jnp.dot(
                grad_ups, wu[:, at], preferred_element_type=F32
            )

        def send_dots():
            with jax.named_scope("dots"):
                ccopy.wait_recv()
                cown[k] = csend[k] + cprecv[k]
                for _, device in peers:
                    remote(cown.at[k], crbuf.at[k, q], cs.at[k], cr.at[k], device).start()
                crbuf[k, q] = cown[k]

        reduce_out(1, k, term, send_dots)

    def bwd_finish(k):
        id_col = idc[k]
        g = gin[k].astype(F32)
        grad_scaled = reduced(1, k)
        c15 = crbuf.at[k, pl.ds(0, chips - 1)]
        with jax.named_scope("dots_wait"):
            remote(c15, c15, cs.at[k], cr.at[k], partner).wait_recv()
        with jax.named_scope("bwd_finish"):
            dots = crbuf[k, 0]
            for n in range(1, chips):
                dots = dots + crbuf[k, n]
            mean = dots.T[:, 0:1] * (1.0 / width)
            scale = inv[k]
            normed = xg[k, :, my_cols].astype(F32) * scale
            grad_normed = grad_scaled * pick(gt_tab[:, my_cols], id_col, members)
            ig[k] = (g + scale * (grad_normed - normed * mean)).astype(BF16)

            @pl.when(s > 0)
            def _():
                hand_on(1, k, ig, gin, gg, below)

            outs_here = g * down[k]
            ins_here = grad_scaled * normed
            for m in range(members):
                mask = id_col == m
                acc_out[m : m + 1, :] += jnp.sum(jnp.where(mask, outs_here, 0.0), axis=0, keepdims=True)
                acc_in[m : m + 1, :] += jnp.sum(jnp.where(mask, ins_here, 0.0), axis=0, keepdims=True)

    @pl.when(s == last)
    def _():
        lax.fori_loop(0, micro, lambda k, carry: (bwd_hidden(k), carry)[1], 0)

    behind = jnp.where(s == last, 0, micro + 2)

    large = [
        pltpu.make_async_copy(v, h, hsem.at[n]) for n, (v, h) in enumerate(((sc, sc_h), (ct, ct_h)))
    ]

    def tick(t, carry):
        u = t - behind

        @pl.when(t < micro)
        def _():
            fwd_arrive(t)

        @pl.when(jnp.logical_and(s < last, jnp.logical_and(u >= 0, u < micro)))
        def _():
            bwd_arrive(u)

        @pl.when(jnp.logical_and(t >= 1, t < micro + 1))
        def _():
            fwd_compute(t - 1)

        @pl.when(jnp.logical_and(s < last, jnp.logical_and(u >= 1, u < micro + 1)))
        def _():
            bwd_hidden(u - 1)

        @pl.when(jnp.logical_and(u >= 1, u < micro + 1))
        def _():
            bwd_compute(u - 1)

        @pl.when(u == micro)
        def _():
            for copy in large:
                copy.start()

        @pl.when(jnp.logical_and(t >= 2, t < micro + 2))
        def _():
            fwd_finish(t - 2)

        @pl.when(jnp.logical_and(u >= 2, u < micro + 2))
        def _():
            bwd_finish(u - 2)

        return carry

    lax.fori_loop(0, 2 * (micro + 2), tick, 0)

    with jax.named_scope("end_send"):
        tables = acc_in[...]
        gtl[0:members, :] = tables * gain[:, my_cols]
        gtl[members : 2 * members, :] = acc_out[...]
        gtl[2 * members : 2 * members + 1, :] = jnp.sum(tables * in_tab[:, my_cols], axis=0, keepdims=True)
        gtab[:, my_cols] = gtl[...]
        for _, device in peers:
            remote(gtl, gtab.at[:, my_cols], osem.at[0], osem.at[1], device).start()

        for kind, src in ((0, ob), (1, ig)):
            for k in range(micro):
                rowf[...] = src[k].astype(F32)
                for n in range(chips):
                    for c in range(2):
                        at = (n * 2 + c) * rows
                        outs[n, (c * 2 + kind) * micro + k] = rowf[at : at + rows, :].astype(BF16)
        for to, device in peers:
            remote(outs.at[to], outr.at[:, :, cols(q, bw)], osem.at[2], osem.at[3], device).start()
        outr[:, :, cols(q, bw)] = outs[q]

    with jax.named_scope("end_turn"):
        hid_t[...] = hid[...].T
        dg_t[...] = dg[...].T
        du_t[...] = du[...].T

    with jax.named_scope("end_wait"):
        most = gtab.at[:, pl.ds(0, (chips - 1) * bw)]
        remote(most, most, osem.at[0], osem.at[1], partner).wait_recv()
        table_part = gtab.at[:, core_cols]
        tables_on = remote(table_part, table_part, osem.at[4], osem.at[5], partner)
        tables_on.start()
        most_outs = outs.at[pl.ds(0, chips - 1)]
        remote(most_outs, most_outs, osem.at[2], osem.at[3], partner).wait_recv()
        rows_on = remote(outr.at[pl.ds(other * 2 * micro, 2 * micro)], outp, osem.at[6], osem.at[7], partner)
        rows_on.start()
        out_x[:, :, core_cols] = outr[pl.ds(core * 2 * micro, micro)]
        out_g[:, :, core_cols] = outr[pl.ds((core * 2 + 1) * micro, micro)]

    with jax.named_scope("end_sent"):
        for k in range(micro):
            for ph in range(2):
                remote(r15(ph, k), r15(ph, k), rs.at[ph, k], rr.at[ph, k], partner).wait_send()
                part = psend.at[ph, k, pl.ds(0, chips // 2)]
                for piece in range(2):
                    remote(part, part, ps.at[ph, k, piece], pr.at[ph, k, piece], partner).wait_send()
            remote(csend.at[k], cprecv.at[k], cps.at[k], cpr.at[k], partner).wait_send()
            c15 = crbuf.at[k, pl.ds(0, chips - 1)]
            remote(c15, c15, cs.at[k], cr.at[k], partner).wait_send()
            half_x = xg.at[k, :, core_cols]
            near_x = rbuf.at[0, k, pl.ds(0, len(near))]
            far_x = rbuf.at[0, k, pl.ds(0, len(far) + 1)]
            remote(half_x, half_x, ds.at[1, k], dr.at[1, k], partner).wait_send()

            @pl.when(s == 0)
            def _():
                most_rows = rg.at[pl.ds(0, chips - 1), k]
                remote(most_rows, most_rows, xs.at[k], xr.at[k], partner).wait_send()
                remote(row_part(k, core), row_part(k, core), xds.at[k], xdr.at[k], partner).wait_send()

            @pl.when(s > 0)
            def _():
                remote(near_x, near_x, ags.at[0, k], agr.at[0, k], partner).wait_send()
                remote(half_x, half_x, ds.at[0, k], dr.at[0, k], partner).wait_send()
                remote(far_x, far_x, zs.at[1, k], zr.at[1, k], below).wait_send()

            @pl.when(s < last)
            def _():
                remote(near_x, near_x, ags.at[1, k], agr.at[1, k], partner).wait_send()
                remote(far_x, far_x, zs.at[0, k], zr.at[0, k], above).wait_send()

            @pl.when(s == last)
            def _():
                remote(r15(1, k), r15(1, k), ags.at[1, k], agr.at[1, k], partner).wait_send()

        @pl.when(s == last)
        def _():
            first.wait_send()
            second.wait_send()

        remote(most, most, osem.at[0], osem.at[1], partner).wait_send()
        remote(most_outs, most_outs, osem.at[2], osem.at[3], partner).wait_send()
        for copy in large:
            copy.wait()
    with jax.named_scope("end_out"):
        tables_on.wait()
        g_in[...] = gtab[0:members, :]
        g_out[...] = gtab[members : 2 * members, :]
        g_gain[...] = gtab[2 * members : 2 * members + 1, :]
        rows_on.wait()
        out_x[:, :, cols(other, half)] = outp[0:micro]
        out_g[:, :, cols(other, half)] = outp[micro : 2 * micro]


def weight_grads(hid, dg, du, sc, ct, *refs):
    gate_out, up_out, down_out = refs[len(refs) // 2 - 1 : len(refs) // 2 + 2]
    small = len(refs) // 2 - 1

    def product(left, right, out):
        out[...] = jnp.dot(left[...], right[...], preferred_element_type=F32).astype(BF16)

    product(dg, sc, gate_out)
    product(du, sc, up_out)
    product(hid, ct, down_out)

    @pl.when(pl.program_id(0) == 0)
    def _():
        for src, dst in zip(refs[:small], refs[small + 3 :]):
            dst[...] = src[...]


def on_device(
    tokens, member_ids, cotangent, w_gate, w_up, w_down, in_scale, mid_scale, out_scale, norm_gain
):
    sections = lax.axis_size("section")
    mps = lax.axis_size("mp")
    places = lax.axis_size("dp") // 2
    chips = places * mps
    micro, rows, width = tokens.shape
    total = member_ids.shape[1]
    members = in_scale.shape[1]
    hidden = w_gate.shape[2]
    half = width // 2
    bw = half // chips
    gate_t = w_gate[0].T
    up_t = w_up[0].T
    down_w = w_down[0]
    all_tokens = micro * total
    vmem = pl.BlockSpec(memory_space=pltpu.VMEM)
    hbm = pl.BlockSpec(memory_space=pl.ANY)
    dma = pltpu.SemaphoreType.DMA

    def buf(*shape, dtype=BF16):
        return pltpu.VMEM(shape, dtype)

    dims = (sections, places, mps, micro, rows, members)
    outs = (
        jax.ShapeDtypeStruct((micro, rows, width), BF16),
        jax.ShapeDtypeStruct((micro, rows, width), BF16),
        jax.ShapeDtypeStruct((hidden, all_tokens), BF16),
        jax.ShapeDtypeStruct((hidden, all_tokens), BF16),
        jax.ShapeDtypeStruct((hidden, all_tokens), BF16),
        jax.ShapeDtypeStruct((all_tokens, width), BF16),
        jax.ShapeDtypeStruct((all_tokens, width), BF16),
        jax.ShapeDtypeStruct((members, width), F32),
        jax.ShapeDtypeStruct((members, width), F32),
        jax.ShapeDtypeStruct((1, width), F32),
        jax.ShapeDtypeStruct((members, hidden), F32),
    )
    out_x, out_g, hid, dg, du, sc, ct, g_in, g_out, g_gain, gmid = pl.pallas_call(
        functools.partial(relay_kernel, dims),
        name="relay",
        out_shape=outs,
        in_specs=[vmem, vmem, vmem, hbm, hbm, hbm, vmem, vmem, vmem, vmem],
        out_specs=[vmem] * 5 + [hbm] * 2 + [vmem] * 4,
        scratch_shapes=[
            buf(all_tokens, hidden), buf(all_tokens, hidden), buf(all_tokens, hidden),
            buf(all_tokens, width), buf(all_tokens, width),
            buf(hidden, width), buf(hidden, width), buf(hidden, width),
            buf(2 * chips, micro, rows, width),
            buf(2 * micro, rows, half),
            buf(chips, 2 * micro, rows, bw),
            buf(total, bw, dtype=F32),
            buf(micro, total, bw), buf(micro, total, bw),
            buf(micro, total, width), buf(micro, total, width),
            buf(members, width, dtype=F32),
            buf(micro, total, 1, dtype=jnp.int32),
            buf(micro, total, 1, dtype=F32),
            buf(2, hidden, total, dtype=F32), buf(micro, hidden, total, dtype=F32),
            buf(micro, total, hidden, dtype=F32), buf(micro, total, hidden, dtype=F32),
            buf(2, micro, chips, total, bw), buf(2, micro, chips, total, bw),
            buf(2, micro, chips, total, bw),
            buf(chips, total, bw, dtype=F32),
            buf(2, micro, chips, total, bw),
            buf(micro, 8, total, dtype=F32), buf(micro, 8, total, dtype=F32),
            buf(micro, 8, total, dtype=F32), buf(micro, chips, 8, total, dtype=F32),
            buf(micro, total, bw, dtype=F32),
            buf(micro, total, bw), buf(micro, total, bw),
            buf(members, bw, dtype=F32), buf(members, bw, dtype=F32),
            buf(16, bw, dtype=F32), buf(16, width, dtype=F32),
            buf(chips, 4 * micro, rows, bw),
            buf(4 * micro, rows, half),
            buf(2 * micro, rows, half),
            dma((3,)), dma((2,)), dma((4,)),
            dma((micro,)), dma((micro,)), dma((micro,)), dma((micro,)),
            dma((2, micro)), dma((2, micro)), dma((2, micro)), dma((2, micro)),
            dma((2, micro)), dma((2, micro)), dma((2, micro, 2)), dma((2, micro, 2)),
            dma((2, micro)), dma((2, micro)),
            dma((micro,)), dma((micro,)), dma((micro,)), dma((micro,)),
            dma((8,)),
        ],
        compiler_params=pltpu.CompilerParams(
            collective_id=0, has_side_effects=True, vmem_limit_bytes=56 * 1024 * 1024
        ),
    )(
        tokens, cotangent, member_ids, gate_t, up_t, down_w,
        in_scale[0], norm_gain, out_scale[0], mid_scale[0],
    )

    step = min(512, width)
    whole = pl.BlockSpec((hidden, all_tokens), lambda n: (0, 0))
    tall = pl.BlockSpec((all_tokens, step), lambda n: (0, n))
    wide = pl.BlockSpec((hidden, step), lambda n: (0, n))
    small = (out_x, out_g, g_in, g_out, g_gain, gmid)
    passed = [pl.BlockSpec(a.shape, lambda n, d=a.ndim: (0,) * d) for a in small]
    grad_gate, grad_up, grad_down, *small = pl.pallas_call(
        weight_grads,
        name="weight_grads",
        grid=(width // step,),
        out_shape=[jax.ShapeDtypeStruct((hidden, width), BF16)] * 3
        + [jax.ShapeDtypeStruct(a.shape, a.dtype) for a in small],
        in_specs=[whole, whole, whole, tall, tall] + passed,
        out_specs=[wide] * 3 + passed,
    )(hid, dg, du, sc, ct, *small)
    out_x, out_g, g_in, g_out, g_gain, gmid = small

    return (
        out_x[None],
        out_g[None],
        grad_gate.T[None],
        grad_up.T[None],
        grad_down[None],
        g_in[None],
        gmid[None],
        g_out[None],
        g_gain,
    )


def solution(mesh):
    in_specs = (
        P(None, ("dp", "mp"), None),
        P(),
        P(None, ("dp", "mp"), None),
        P("section", None, ("dp", "mp")),
        P("section", None, ("dp", "mp")),
        P("section", ("dp", "mp"), None),
        P("section", None, None),
        P("section", None, ("dp", "mp")),
        P("section", None, None),
        P("section", None),
    )
    out_specs = (
        P("section", None, ("dp", "mp"), None),
        P("section", None, ("dp", "mp"), None),
        P("section", None, ("dp", "mp")),
        P("section", None, ("dp", "mp")),
        P("section", ("dp", "mp"), None),
        P("section", None, None),
        P("section", None, ("dp", "mp")),
        P("section", None, None),
        P("section", None),
    )
    return jax.shard_map(
        on_device, mesh=mesh, in_specs=in_specs, out_specs=out_specs, check_vma=False
    )
```

time: 255 us -> 189 us (0.74)
  Pallas kernels: 236 us -> 188 us
  matrix products: 10.4 us -> 0 us
  local copies, waits for them, and re-layouts: 7.04 us -> 0 us
    pallas_call x1, Pallas kernels: 236 us -> 178 us  [on_device(): pl.pallas_call(functools.partial(relay_kernel, dims), name='relay', out_s...]
    dot_general x3 -> x0, matrix products: 10.4 us -> none  [weight_grad(): lax.dot_general(left, right, (((0,), (0,)), ((), ())), preferred_element_...]
    pallas_call x0 -> x1, Pallas kernels: none -> 9.95 us  [on_device(): pl.pallas_call(weight_grads, name='weight_grads', grid=(width // step,),...]
    broadcast_in_dim x2 -> x0, local copies, waits for them, and re-layouts: 3.31 us -> none  [the longest x1 1.66 us: on_device(): out[micro:][None]]
where the time goes in v2:
time: 189 us
  Pallas kernels  188 us (99%)
    pallas_call x1, Pallas kernels, on_device(): pl.pallas_call(functools.partial(relay_kernel, dims), name='relay', out_s...  178 us
    pallas_call x1, Pallas kernels, on_device(): pl.pallas_call(weight_grads, name='weight_grads', grid=(width // step,),...  9.95 us

profile of v2, /device:TPU:1, one launch (start us, length us, event | category | flops | bytes accessed | tf_op | source)
XLA Modules:
  0.0 188.7 jit_solution(3517760479413423754)
XLA Ops:
  0.6 178.1 %relay.1 = (bf16[3,2,4096]{2,1,0:T(2,128)(2,1)}, bf16[3,2,4096]{2,1,0:T(2,128)(2,1)}, bf16[448,192]{1,0:T(8,128)(2,1)}, bf16[448,192]{1,0:T(8,128)(2,1)}, bf16[4...) custom-call(bf16[3,2,4096]{2,1,0:T(2,128)(2,1)} %tok.1, ...), custom_call_target="tpu_custom_call" | custom-call | tf_op jit(solution)/shard_map/relay/pallas_call | solution.py:651
  178.8 10.0 %weight_grads.1 = (bf16[448,4096]{1,0:T(8,128)(2,1)}, bf16[448,4096]{1,0:T(8,128)(2,1)}, bf16[448,4096]{1,0:T(8,128)(2,1)}, bf16[3,2,4096]{2,1,0:T(2,128)(2,1)},...) custom-call(bf16[448,192]{1,0:T(8,128)(2,1)} %get-tuple-element.29.h, ...), custom_call_target="tpu_custom_call" | custom-call | tf_op jit(solution)/shard_map/weight_grads/pallas_call | solution.py:707

commit v3 on v2

--- a/solution.py
+++ b/solution.py
@@ -26,13 +26,14 @@
 
 def relay_kernel(
     dims,
-    tok, cot, ids, wg_h, wu_h, wd_h, in_tab, gain, out_tab, mid_tab,
-    out_x, out_g, hid_t, dg_t, du_t, sc_h, ct_h, g_in, g_out, g_gain, gmid,
-    hid, dg, du, sc, ct,
+    tok_h, cot_h, ids_h, in_h, gain_h, out_h, mid_h, wg_h, wu_h, wd_h,
+    out_x, out_g, g_gate, g_up, g_down, g_in, g_out, g_gain, gmid,
+    tok, cot, ids, in_tab, gain, out_tab, mid_tab, in_rows, out_rows,
+    hid, dg, du, sc, ct, turned,
     wg, wu, wd, rg, t1, initr, rowf, xin, gin, xg, gg, gt_tab, idc, inv, pacc, phid, gpre, upre,
     psend, precv, pown, pf, rbuf, csend, cprecv, cown, crbuf, down, ob, ig,
     acc_in, acc_out, gtl, gtab, outs, outr, outp,
-    wsem, hsem, isem, xs, xr, xds, xdr, zs, zr, ags, agr, ds, dr, ps, pr, rs, rr, cps, cpr, cs, cr, osem,
+    insem, wsem, isem, xs, xr, xds, xdr, zs, zr, ags, agr, ds, dr, ps, pr, rs, rr, cps, cpr, cs, cr, osem,
 ):
     sections, places, mps, micro, rows, members = dims
     chips = places * mps
@@ -77,8 +78,8 @@
     far = [p for p, d in zip(peers, offsets) if hops(d) > reach]
     near = [p for p, d in zip(peers, offsets) if hops(d) <= reach]
     groups = [
+        [p for p, d in zip(peers, offsets) if d[1] % 2 == 0],
         [p for p, d in zip(peers, offsets) if d[1] % 2 == 1],
-        [p for p, d in zip(peers, offsets) if d[1] % 2 == 0],
     ]
 
     def remote(src, dst, send, recv, device):
@@ -90,6 +91,17 @@
     def cols(index, size):
         return pl.ds(pl.multiple_of(index * size, size), size)
 
+    inputs = [
+        pltpu.make_async_copy(h, v, insem.at[i])
+        for i, (h, v) in enumerate(
+            (
+                (tok_h, tok), (cot_h, cot), (ids_h, ids), (in_h, in_tab),
+                (gain_h, gain), (out_h, out_tab), (mid_h, mid_tab),
+            )
+        )
+    ]
+    for copy in inputs:
+        copy.start()
     weights = [
         pltpu.make_async_copy(h, v, wsem.at[i])
         for i, (h, v) in enumerate(((wg_h, wg), (wu_h, wu), (wd_h, wd)))
@@ -97,6 +109,8 @@
     for copy in weights:
         copy.start()
 
+    init_scope = jax.named_scope("init_local")
+    init_scope.__enter__()
     barrier = pltpu.get_barrier_semaphore()
     for _, device in peers:
         pl.semaphore_signal(barrier, inc=1, device_id=device, device_id_type=pl.DeviceIdType.MESH)
@@ -112,6 +126,51 @@
         for device in [below] + [{**d, **below} for _, d in far]:
             pl.semaphore_signal(barrier, inc=1, device_id=device, device_id_type=pl.DeviceIdType.MESH)
 
+    for copy in inputs:
+        copy.wait()
+    init_scope.__exit__(None, None, None)
+    links = (s < last).astype(jnp.int32) + (s > 0).astype(jnp.int32)
+    with jax.named_scope("init_barrier"):
+        pl.semaphore_wait(barrier, chips + (1 + len(far)) * links)
+
+    my_cols = cols(block, bw)
+    core_cols = cols(core, half)
+    r15 = lambda ph, k: rbuf.at[ph, k, pl.ds(0, chips - 1)]
+
+    def spread(ph, k, src, dst, targets):
+        for _, device in targets:
+            remote(src.at[k], dst.at[k, :, my_cols], ags.at[ph, k], agr.at[ph, k], device).start()
+        dst[k, :, my_cols] = src[k]
+
+    def hand_on(ph, k, src, dst, gathered, section):
+        remote(src.at[k], dst.at[k], zs.at[ph, k], zr.at[ph, k], section).start()
+        for _, device in far:
+            remote(
+                src.at[k], gathered.at[k, :, my_cols], zs.at[ph, k], agr.at[ph, k], {**device, **section}
+            ).start()
+
+    row_part = lambda k, c: rg.at[pl.ds(c * chips, chips), k]
+
+    @pl.when(s == 0)
+    def _():
+        for k in range(micro):
+            for _, device in peers:
+                remote(tok.at[k], rg.at[block, k], xs.at[k], xr.at[k], device).start()
+            rg[block, k] = tok[k]
+
+    def forward_rows(k):
+        most_rows = rg.at[pl.ds(0, chips - 1), k]
+        remote(most_rows, most_rows, xs.at[k], xr.at[k], partner).wait_recv()
+        remote(row_part(k, core), row_part(k, core), xds.at[k], xdr.at[k], partner).start()
+
+    def place_rows(k):
+        remote(row_part(k, other), row_part(k, other), xds.at[k], xdr.at[k], partner).wait_recv()
+        for c in range(2):
+            for n in range(chips):
+                at = (n * 2 + c) * rows
+                xg[k, at : at + rows, :] = rg[c * chips + n, k]
+
+    chunk = min(512, half)
     gt_tab[...] = in_tab[...] * gain[...]
     acc_in[...] = jnp.zeros_like(acc_in)
     acc_out[...] = jnp.zeros_like(acc_out)
@@ -125,45 +184,11 @@
     for k in range(micro):
         picked = jnp.where(source == j, jnp.broadcast_to(ids[k : k + 1, :], (total, total)), 0)
         idc[k] = jnp.sum(picked.astype(F32), axis=1, keepdims=True).astype(jnp.int32)
-    links = (s < last).astype(jnp.int32) + (s > 0).astype(jnp.int32)
-    pl.semaphore_wait(barrier, chips + (1 + len(far)) * links)
-
-    my_cols = cols(block, bw)
-    core_cols = cols(core, half)
-    r15 = lambda ph, k: rbuf.at[ph, k, pl.ds(0, chips - 1)]
-
-    def spread(ph, k, src, dst, targets):
-        for _, device in targets:
-            remote(src.at[k], dst.at[k, :, my_cols], ags.at[ph, k], agr.at[ph, k], device).start()
-        dst[k, :, my_cols] = src[k]
-
-    def hand_on(ph, k, src, dst, gathered, section):
-        remote(src.at[k], dst.at[k], zs.at[ph, k], zr.at[ph, k], section).start()
-        for _, device in far:
-            remote(
-                src.at[k], gathered.at[k, :, my_cols], zs.at[ph, k], agr.at[ph, k], {**device, **section}
-            ).start()
-
-    row_part = lambda k, c: rg.at[pl.ds(c * chips, chips), k]
-
-    @pl.when(s == 0)
-    def _():
-        for k in range(micro):
-            for _, device in peers:
-                remote(tok.at[k], rg.at[block, k], xs.at[k], xr.at[k], device).start()
-            rg[block, k] = tok[k]
-
-    def forward_rows(k):
-        most_rows = rg.at[pl.ds(0, chips - 1), k]
-        remote(most_rows, most_rows, xs.at[k], xr.at[k], partner).wait_recv()
-        remote(row_part(k, core), row_part(k, core), xds.at[k], xdr.at[k], partner).start()
-
-    def place_rows(k):
-        remote(row_part(k, other), row_part(k, other), xds.at[k], xdr.at[k], partner).wait_recv()
-        for c in range(2):
-            for n in range(chips):
-                at = (n * 2 + c) * rows
-                xg[k, at : at + rows, :] = rg[c * chips + n, k]
+    for k in range(micro):
+        for at in range(0, width, chunk):
+            here = slice(at, at + chunk)
+            in_rows[k, :, here] = pick(gt_tab[:, here], idc[k], members)
+            out_rows[k, :, here] = pick(out_tab[:, here], idc[k], members)
 
     mine = pl.ds(core * micro, micro)
     first = remote(cot.at[:, :, cols(other, half)], t1.at[mine], isem.at[0], isem.at[1], partner)
@@ -187,10 +212,10 @@
             gin[k] = rowf[...].astype(BF16)
             spread(1, k, gin, gg, peers)
 
-    for copy in weights:
-        copy.wait()
-
-    chunk = min(512, half)
+    with jax.named_scope("init_weights"):
+        for copy in weights:
+            copy.wait()
+
     pieces = [(at, min(256, hidden - at)) for at in range(0, hidden, 256)]
 
     def part_cols(c, n, size):
@@ -205,7 +230,7 @@
         halves = half // 2 // step
         copies = []
         for piece in range(2):
-            low = 1 - y_low if piece == 0 else y_low
+            low = y_low if piece == 0 else 1 - y_low
             with jax.named_scope("down_other"):
                 for n in range(halves):
                     at = other * half + low * (half // 2) + n * step
@@ -227,7 +252,7 @@
         if between is not None:
             between()
         for piece in range(2):
-            low = 1 - y_low if piece == 0 else y_low
+            low = y_low if piece == 0 else 1 - y_low
             with jax.named_scope("partner_wait"):
                 copies[piece].wait_recv()
             with jax.named_scope("combine"):
@@ -249,6 +274,10 @@
     def token_rows(k):
         return pl.ds(pl.multiple_of(k * total, total), total)
 
+    def member_sums(acc, id_col, value):
+        for m in range(members):
+            acc[m : m + 1, :] += jnp.sum(jnp.where(id_col == m, value, 0.0), axis=0, keepdims=True)
+
     def fwd_arrive(k):
         with jax.named_scope("x_wait"):
             @pl.when(s > 0)
@@ -268,7 +297,7 @@
             def step(n, carry):
                 at = part_cols(c, n, chunk)
                 x = xg[k, :, at].astype(F32)
-                sc[here, at] = (x * pick(gt_tab[:, at], id_col, members)).astype(BF16)
+                sc[here, at] = (x * in_rows[k, :, at]).astype(BF16)
                 x2 = x * x
                 for e in range(chunk // 128):
                     carry = carry + x2[:, e * 128 : (e + 1) * 128]
@@ -317,14 +346,16 @@
                 upre[k, :, hs] = up
                 product = gate / (1.0 + jnp.exp(-gate)) * up
                 hid[here, hs] = (product * pick(mid_tab[:, hs], id_col, members)).astype(BF16)
-        h = hid[here, :]
+
+    def fwd_down(k):
+        h = hid[token_rows(k), :]
         reduce_out(0, k, lambda at: jnp.dot(h, wd[:, at], preferred_element_type=F32))
 
     def fwd_finish(k):
         value = reduced(0, k)
         with jax.named_scope("fwd_finish"):
             x = xg[k, :, my_cols].astype(F32)
-            ob[k] = (x + value * pick(out_tab[:, my_cols], idc[k], members)).astype(BF16)
+            ob[k] = (x + value * out_rows[k, :, my_cols]).astype(BF16)
 
             @pl.when(s < last)
             def _():
@@ -340,13 +371,12 @@
 
     def bwd_hidden(k):
         here = token_rows(k)
-        id_col = idc[k]
 
         def cot_half(c):
             def step(n, carry):
                 at = part_cols(c, n, chunk)
                 g = gg[k, :, at].astype(F32)
-                ct[here, at] = (g * pick(out_tab[:, at], id_col, members)).astype(BF16)
+                ct[here, at] = (g * out_rows[k, :, at]).astype(BF16)
                 return carry
 
             lax.fori_loop(0, half // chunk, step, 0)
@@ -436,32 +466,41 @@
             mean = dots.T[:, 0:1] * (1.0 / width)
             scale = inv[k]
             normed = xg[k, :, my_cols].astype(F32) * scale
-            grad_normed = grad_scaled * pick(gt_tab[:, my_cols], id_col, members)
+            grad_normed = grad_scaled * in_rows[k, :, my_cols]
             ig[k] = (g + scale * (grad_normed - normed * mean)).astype(BF16)
 
             @pl.when(s > 0)
             def _():
                 hand_on(1, k, ig, gin, gg, below)
 
-            outs_here = g * down[k]
-            ins_here = grad_scaled * normed
-            for m in range(members):
-                mask = id_col == m
-                acc_out[m : m + 1, :] += jnp.sum(jnp.where(mask, outs_here, 0.0), axis=0, keepdims=True)
-                acc_in[m : m + 1, :] += jnp.sum(jnp.where(mask, ins_here, 0.0), axis=0, keepdims=True)
+            member_sums(acc_in, id_col, grad_scaled * normed)
+
+    def out_scale_grad(k):
+        member_sums(acc_out, idc[k], gin[k].astype(F32) * down[k])
 
     @pl.when(s == last)
     def _():
         lax.fori_loop(0, micro, lambda k, carry: (bwd_hidden(k), carry)[1], 0)
 
     behind = jnp.where(s == last, 0, micro + 2)
-
-    large = [
-        pltpu.make_async_copy(v, h, hsem.at[n]) for n, (v, h) in enumerate(((sc, sc_h), (ct, ct_h)))
-    ]
+    down_behind = jnp.where(s == last, micro + 2, 1)
+
+    def weight_grads():
+        wide = min(1024, width)
+        with jax.named_scope("weight_grads"):
+            for left, right, out in ((dg, sc, g_gate), (du, sc, g_up), (hid, ct, g_down)):
+                turned[...] = left[...].T
+
+                def step(n, carry):
+                    at = cols(n, wide)
+                    out[:, at] = jnp.dot(turned[...], right[:, at], preferred_element_type=F32).astype(BF16)
+                    return carry
+
+                lax.fori_loop(0, width // wide, step, 0)
 
     def tick(t, carry):
         u = t - behind
+        d = t - down_behind
 
         @pl.when(t < micro)
         def _():
@@ -475,6 +514,10 @@
         def _():
             fwd_compute(t - 1)
 
+        @pl.when(jnp.logical_and(d >= 0, d < micro))
+        def _():
+            fwd_down(d)
+
         @pl.when(jnp.logical_and(s < last, jnp.logical_and(u >= 1, u < micro + 1)))
         def _():
             bwd_hidden(u - 1)
@@ -483,18 +526,29 @@
         def _():
             bwd_compute(u - 1)
 
-        @pl.when(u == micro)
-        def _():
-            for copy in large:
-                copy.start()
-
-        @pl.when(jnp.logical_and(t >= 2, t < micro + 2))
-        def _():
-            fwd_finish(t - 2)
+        @pl.when(jnp.logical_and(s == 0, u == micro + 1))
+        def _():
+            weight_grads()
+
+        @pl.when(jnp.logical_and(d >= 1, d < micro + 1))
+        def _():
+            fwd_finish(d - 1)
+
+        @pl.when(jnp.logical_and(s == last, jnp.logical_and(d >= 1, d < micro + 1)))
+        def _():
+            out_scale_grad(d - 1)
 
         @pl.when(jnp.logical_and(u >= 2, u < micro + 2))
         def _():
             bwd_finish(u - 2)
+
+        @pl.when(jnp.logical_and(s < last, jnp.logical_and(u >= 2, u < micro + 2)))
+        def _():
+            out_scale_grad(u - 2)
+
+        @pl.when(jnp.logical_and(s > 0, u == micro + 1))
+        def _():
+            weight_grads()
 
         return carry
 
@@ -519,11 +573,6 @@
         for to, device in peers:
             remote(outs.at[to], outr.at[:, :, cols(q, bw)], osem.at[2], osem.at[3], device).start()
         outr[:, :, cols(q, bw)] = outs[q]
-
-    with jax.named_scope("end_turn"):
-        hid_t[...] = hid[...].T
-        dg_t[...] = dg[...].T
-        du_t[...] = du[...].T
 
     with jax.named_scope("end_wait"):
         most = gtab.at[:, pl.ds(0, (chips - 1) * bw)]
@@ -581,8 +630,6 @@
 
         remote(most, most, osem.at[0], osem.at[1], partner).wait_send()
         remote(most_outs, most_outs, osem.at[2], osem.at[3], partner).wait_send()
-        for copy in large:
-            copy.wait()
     with jax.named_scope("end_out"):
         tables_on.wait()
         g_in[...] = gtab[0:members, :]
@@ -593,21 +640,16 @@
         out_g[:, :, cols(other, half)] = outp[micro : 2 * micro]
 
 
-def weight_grads(hid, dg, du, sc, ct, *refs):
-    gate_out, up_out, down_out = refs[len(refs) // 2 - 1 : len(refs) // 2 + 2]
-    small = len(refs) // 2 - 1
-
-    def product(left, right, out):
-        out[...] = jnp.dot(left[...], right[...], preferred_element_type=F32).astype(BF16)
-
-    product(dg, sc, gate_out)
-    product(du, sc, up_out)
-    product(hid, ct, down_out)
-
-    @pl.when(pl.program_id(0) == 0)
-    def _():
-        for src, dst in zip(refs[:small], refs[small + 3 :]):
-            dst[...] = src[...]
+def deliver(count, *refs):
+    sems = refs[-1]
+    copies = [
+        pltpu.make_async_copy(src, dst, sems.at[n])
+        for n, (src, dst) in enumerate(zip(refs[:count], refs[count : 2 * count]))
+    ]
+    for copy in copies:
+        copy.start()
+    for copy in copies:
+        copy.wait()
 
 
 def on_device(
@@ -636,27 +678,29 @@
 
     dims = (sections, places, mps, micro, rows, members)
     outs = (
-        jax.ShapeDtypeStruct((micro, rows, width), BF16),
-        jax.ShapeDtypeStruct((micro, rows, width), BF16),
-        jax.ShapeDtypeStruct((hidden, all_tokens), BF16),
-        jax.ShapeDtypeStruct((hidden, all_tokens), BF16),
-        jax.ShapeDtypeStruct((hidden, all_tokens), BF16),
-        jax.ShapeDtypeStruct((all_tokens, width), BF16),
-        jax.ShapeDtypeStruct((all_tokens, width), BF16),
-        jax.ShapeDtypeStruct((members, width), F32),
-        jax.ShapeDtypeStruct((members, width), F32),
-        jax.ShapeDtypeStruct((1, width), F32),
-        jax.ShapeDtypeStruct((members, hidden), F32),
+        pltpu.VMEM((micro, rows, width), BF16),
+        pltpu.VMEM((micro, rows, width), BF16),
+        pltpu.VMEM((hidden, width), BF16),
+        pltpu.VMEM((hidden, width), BF16),
+        pltpu.VMEM((hidden, width), BF16),
+        pltpu.VMEM((members, width), F32),
+        pltpu.VMEM((members, width), F32),
+        pltpu.VMEM((1, width), F32),
+        pltpu.VMEM((members, hidden), F32),
     )
-    out_x, out_g, hid, dg, du, sc, ct, g_in, g_out, g_gain, gmid = pl.pallas_call(
+    results = pl.pallas_call(
         functools.partial(relay_kernel, dims),
         name="relay",
         out_shape=outs,
-        in_specs=[vmem, vmem, vmem, hbm, hbm, hbm, vmem, vmem, vmem, vmem],
-        out_specs=[vmem] * 5 + [hbm] * 2 + [vmem] * 4,
+        in_specs=[pl.BlockSpec(memory_space=pltpu.HBM)] * 10,
+        out_specs=[vmem] * len(outs),
         scratch_shapes=[
+            buf(micro, rows, width), buf(micro, rows, width), buf(micro, total, dtype=jnp.int32),
+            buf(members, width, dtype=F32), buf(1, width, dtype=F32),
+            buf(members, width, dtype=F32), buf(members, hidden, dtype=F32),
+            buf(micro, total, width, dtype=F32), buf(micro, total, width, dtype=F32),
             buf(all_tokens, hidden), buf(all_tokens, hidden), buf(all_tokens, hidden),
-            buf(all_tokens, width), buf(all_tokens, width),
+            buf(all_tokens, width), buf(all_tokens, width), buf(hidden, all_tokens),
             buf(hidden, width), buf(hidden, width), buf(hidden, width),
             buf(2 * chips, micro, rows, width),
             buf(2 * micro, rows, half),
@@ -682,7 +726,7 @@
             buf(chips, 4 * micro, rows, bw),
             buf(4 * micro, rows, half),
             buf(2 * micro, rows, half),
-            dma((3,)), dma((2,)), dma((4,)),
+            dma((7,)), dma((3,)), dma((4,)),
             dma((micro,)), dma((micro,)), dma((micro,)), dma((micro,)),
             dma((2, micro)), dma((2, micro)), dma((2, micro)), dma((2, micro)),
             dma((2, micro)), dma((2, micro)), dma((2, micro, 2)), dma((2, micro, 2)),
@@ -691,29 +735,22 @@
             dma((8,)),
         ],
         compiler_params=pltpu.CompilerParams(
-            collective_id=0, has_side_effects=True, vmem_limit_bytes=56 * 1024 * 1024
+            collective_id=0, has_side_effects=True, vmem_limit_bytes=46 * 1024 * 1024
         ),
     )(
-        tokens, cotangent, member_ids, gate_t, up_t, down_w,
-        in_scale[0], norm_gain, out_scale[0], mid_scale[0],
+        tokens, cotangent, member_ids, in_scale[0], norm_gain, out_scale[0], mid_scale[0],
+        gate_t, up_t, down_w,
     )
 
-    step = min(512, width)
-    whole = pl.BlockSpec((hidden, all_tokens), lambda n: (0, 0))
-    tall = pl.BlockSpec((all_tokens, step), lambda n: (0, n))
-    wide = pl.BlockSpec((hidden, step), lambda n: (0, n))
-    small = (out_x, out_g, g_in, g_out, g_gain, gmid)
-    passed = [pl.BlockSpec(a.shape, lambda n, d=a.ndim: (0,) * d) for a in small]
-    grad_gate, grad_up, grad_down, *small = pl.pallas_call(
-        weight_grads,
-        name="weight_grads",
-        grid=(width // step,),
-        out_shape=[jax.ShapeDtypeStruct((hidden, width), BF16)] * 3
-        + [jax.ShapeDtypeStruct(a.shape, a.dtype) for a in small],
-        in_specs=[whole, whole, whole, tall, tall] + passed,
-        out_specs=[wide] * 3 + passed,
-    )(hid, dg, du, sc, ct, *small)
-    out_x, out_g, g_in, g_out, g_gain, gmid = small
+    out_x, out_g, grad_gate, grad_up, grad_down, g_in, g_out, g_gain, gmid = pl.pallas_call(
+        functools.partial(deliver, len(outs)),
+        name="deliver",
+        out_shape=[jax.ShapeDtypeStruct(o.shape, o.dtype) for o in outs],
+        in_specs=[vmem] * len(outs),
+        out_specs=[hbm] * len(outs),
+        scratch_shapes=[dma((len(outs),))],
+        compiler_params=pltpu.CompilerParams(vmem_limit_bytes=1024 * 1024),
+    )(*[pltpu.with_memory_space_constraint(r, pltpu.VMEM) for r in results])
 
     return (
         out_x[None],

time: 189 us -> 174 us (0.921)
  Pallas kernels: 188 us -> 173 us
    pallas_call x1, Pallas kernels: 178 us -> 169 us  [on_device(): pl.pallas_call(functools.partial(relay_kernel, dims), name='relay', out_s...]
    pallas_call x1, Pallas kernels: 9.95 us -> 4.38 us  [on_device(): pl.pallas_call(functools.partial(deliver, len(outs)), name='deliver', out...]
where the time goes in v3:
time: 174 us
  Pallas kernels  173 us (99%)
    pallas_call x1, Pallas kernels, on_device(): pl.pallas_call(functools.partial(relay_kernel, dims), name='relay', out_s...  169 us
    pallas_call x1, Pallas kernels, on_device(): pl.pallas_call(functools.partial(deliver, len(outs)), name='deliver', out...  4.38 us

profile of v3, /device:TPU:1, one launch (start us, length us, event | category | flops | bytes accessed | tf_op | source)
XLA Modules:
  0.0 173.9 jit_solution(16946015746796496887)
XLA Ops:
  0.6 168.7 %relay.1 = (bf16[3,2,4096]{2,1,0:T(2,128)(2,1)S(1)}, bf16[3,2,4096]{2,1,0:T(2,128)(2,1)S(1)}, bf16[448,4096]{1,0:T(8,128)(2,1)S(1)}, bf16[448,4096]{1,0:T(8,128)...) custom-call(bf16[3,2,4096]{2,1,0:T(2,128)(2,1)} %tok_h.1, ...), custom_call_target="tpu_custom_call" | custom-call | tf_op jit(solution)/shard_map/relay/pallas_call | solution.py:691
  169.3 4.4 %deliver.1 = (bf16[3,2,4096]{2,1,0:T(2,128)(2,1)}, bf16[3,2,4096]{2,1,0:T(2,128)(2,1)}, bf16[448,4096]{1,0:T(8,128)(2,1)}, bf16[448,4096]{1,0:T(8,128)(2,1)}, bf...) custom-call(bf16[3,2,4096]{2,1,0:T(2,128)(2,1)S(1)} %get-tuple-eleme, ...), custom_call_target="tpu_custom_call" | custom-call | tf_op jit(solution)/shard_map/deliver/pallas_call | solution.py:745

commit v4 on v3

--- a/solution.py
+++ b/solution.py
@@ -29,8 +29,8 @@
     tok_h, cot_h, ids_h, in_h, gain_h, out_h, mid_h, wg_h, wu_h, wd_h,
     out_x, out_g, g_gate, g_up, g_down, g_in, g_out, g_gain, gmid,
     tok, cot, ids, in_tab, gain, out_tab, mid_tab, in_rows, out_rows,
-    hid, dg, du, sc, ct, turned,
-    wg, wu, wd, rg, t1, initr, rowf, xin, gin, xg, gg, gt_tab, idc, inv, pacc, phid, gpre, upre,
+    hid, dg, du, sc, ct, turned, ggate, gup, gmids,
+    wgu, wd, rg, t1, initr, rowf, xin, gin, xg, gg, gt_tab, idc, inv, pacc, phid, gpre, upre,
     psend, precv, pown, pf, rbuf, csend, cprecv, cown, crbuf, down, ob, ig,
     acc_in, acc_out, gtl, gtab, outs, outr, outp,
     insem, wsem, isem, xs, xr, xds, xdr, zs, zr, ags, agr, ds, dr, ps, pr, rs, rr, cps, cpr, cs, cr, osem,
@@ -65,8 +65,11 @@
         return min(d[0], across - d[0]) + min(d[1], 2 * mps - d[1])
 
     offsets = [(dx, dy) for dx in range(across) for dy in range(2 * mps) if dx or dy]
-    offsets.sort(key=lambda d: -hops(d))
-    reach = hops(offsets[0]) // 2
+    def ups(d):
+        return (d[0] if d[0] * 2 <= across else 0) + (d[1] if d[1] <= mps else 0)
+
+    offsets.sort(key=lambda d: (-ups(d), -hops(d)))
+    reach = max(map(hops, offsets)) // 2
 
     def chip(dx, dy):
         x = lax.rem(along_x + dx, across)
@@ -91,6 +94,8 @@
     def cols(index, size):
         return pl.ds(pl.multiple_of(index * size, size), size)
 
+    wg = wgu.at[0:hidden]
+    wu = wgu.at[hidden : 2 * hidden]
     inputs = [
         pltpu.make_async_copy(h, v, insem.at[i])
         for i, (h, v) in enumerate(
@@ -109,8 +114,6 @@
     for copy in weights:
         copy.start()
 
-    init_scope = jax.named_scope("init_local")
-    init_scope.__enter__()
     barrier = pltpu.get_barrier_semaphore()
     for _, device in peers:
         pl.semaphore_signal(barrier, inc=1, device_id=device, device_id_type=pl.DeviceIdType.MESH)
@@ -126,9 +129,9 @@
         for device in [below] + [{**d, **below} for _, d in far]:
             pl.semaphore_signal(barrier, inc=1, device_id=device, device_id_type=pl.DeviceIdType.MESH)
 
-    for copy in inputs:
-        copy.wait()
-    init_scope.__exit__(None, None, None)
+    with jax.named_scope("init_local"):
+        for copy in inputs:
+            copy.wait()
     links = (s < last).astype(jnp.int32) + (s > 0).astype(jnp.int32)
     with jax.named_scope("init_barrier"):
         pl.semaphore_wait(barrier, chips + (1 + len(far)) * links)
@@ -328,11 +331,6 @@
             @pl.when(s > 0)
             def _():
                 copy.wait_recv()
-
-            @pl.when(jnp.logical_and(s == 0, k < micro - 1))
-            def _():
-                forward_rows(jnp.minimum(k + 1, micro - 1))
-
         with jax.named_scope("gateup_other"):
             squares = scaled_half(other, squares)
             scale = lax.rsqrt(jnp.sum(squares, axis=-1, keepdims=True) * (1.0 / width) + EPS)
@@ -348,6 +346,10 @@
                 hid[here, hs] = (product * pick(mid_tab[:, hs], id_col, members)).astype(BF16)
 
     def fwd_down(k):
+        @pl.when(jnp.logical_and(s == 0, k < micro - 1))
+        def _():
+            forward_rows(jnp.minimum(k + 1, micro - 1))
+
         h = hid[token_rows(k), :]
         reduce_out(0, k, lambda at: jnp.dot(h, wd[:, at], preferred_element_type=F32))
 
@@ -407,7 +409,7 @@
         with jax.named_scope("grads"):
             scale = inv[k]
             dots = jnp.zeros((total, 1), F32)
-            grad_gates = []
+            grad_pre = []
             grad_ups = []
             for h, size in pieces:
                 hs = slice(h, h + size)
@@ -416,31 +418,26 @@
                 up = upre[k, :, hs]
                 sig = 1.0 / (1.0 + jnp.exp(-gate))
                 silu = gate * sig
-                mids = grad_hidden * (silu * up)
-                for m in range(members):
-                    gmid[m : m + 1, hs] += jnp.sum(jnp.where(id_col == m, mids, 0.0), axis=0, keepdims=True)
                 grad_product = grad_hidden * pick(mid_tab[:, hs], id_col, members)
                 grad_gate = grad_product * up * sig * (1.0 + gate * (1.0 - sig))
                 grad_up = grad_product * silu
-                dg[here, hs] = (grad_gate * scale).astype(BF16)
-                du[here, hs] = (grad_up * scale).astype(BF16)
+                ggate[:, hs] = grad_gate
+                gup[:, hs] = grad_up
+                gmids[:, hs] = grad_hidden * (silu * up)
                 grad_gate = grad_gate.astype(BF16)
                 grad_up = grad_up.astype(BF16)
-                grad_gates.append(grad_gate)
+                grad_pre.append(grad_gate)
                 grad_ups.append(grad_up)
                 dots = dots + jnp.sum(
                     grad_gate.astype(F32) * gate + grad_up.astype(F32) * up, axis=-1, keepdims=True
                 )
-            csend[k] = jnp.broadcast_to(dots, (total, 128)).T[0:8, :]
+            csend[k] = jnp.broadcast_to(dots, (total, 128)).T[0:1, :]
             ccopy = remote(csend.at[k], cprecv.at[k], cps.at[k], cpr.at[k], partner)
             ccopy.start()
-            grad_gates = jnp.concatenate(grad_gates, axis=1)
-            grad_ups = jnp.concatenate(grad_ups, axis=1)
+            pre = jnp.concatenate(grad_pre + grad_ups, axis=1)
 
         def term(at):
-            return jnp.dot(grad_gates, wg[:, at], preferred_element_type=F32) + jnp.dot(
-                grad_ups, wu[:, at], preferred_element_type=F32
-            )
+            return jnp.dot(pre, wgu[:, at], preferred_element_type=F32)
 
         def send_dots():
             with jax.named_scope("dots"):
@@ -449,25 +446,30 @@
                 for _, device in peers:
                     remote(cown.at[k], crbuf.at[k, q], cs.at[k], cr.at[k], device).start()
                 crbuf[k, q] = cown[k]
+            with jax.named_scope("keep"):
+                dg[here, :] = (ggate[...] * scale).astype(BF16)
+                du[here, :] = (gup[...] * scale).astype(BF16)
+                member_sums(gmid, id_col, gmids[...])
 
         reduce_out(1, k, term, send_dots)
 
     def bwd_finish(k):
         id_col = idc[k]
-        g = gin[k].astype(F32)
-        grad_scaled = reduced(1, k)
         c15 = crbuf.at[k, pl.ds(0, chips - 1)]
         with jax.named_scope("dots_wait"):
             remote(c15, c15, cs.at[k], cr.at[k], partner).wait_recv()
-        with jax.named_scope("bwd_finish"):
             dots = crbuf[k, 0]
             for n in range(1, chips):
                 dots = dots + crbuf[k, n]
-            mean = dots.T[:, 0:1] * (1.0 / width)
+            mean = jnp.broadcast_to(dots, (8, total)).T[:, 0:1] * (1.0 / width)
             scale = inv[k]
+            g = gin[k].astype(F32)
             normed = xg[k, :, my_cols].astype(F32) * scale
+            kept = g - scale * mean * normed
+        grad_scaled = reduced(1, k)
+        with jax.named_scope("bwd_finish"):
             grad_normed = grad_scaled * in_rows[k, :, my_cols]
-            ig[k] = (g + scale * (grad_normed - normed * mean)).astype(BF16)
+            ig[k] = (kept + scale * grad_normed).astype(BF16)
 
             @pl.when(s > 0)
             def _():
@@ -498,6 +500,20 @@
 
                 lax.fori_loop(0, width // wide, step, 0)
 
+    def send_rows(kind, src):
+        for k in range(micro):
+            rowf[...] = src[k].astype(F32)
+            for n in range(chips):
+                for c in range(2):
+                    at = (n * 2 + c) * rows
+                    outs[kind, n, c * micro + k] = rowf[at : at + rows, :].astype(BF16)
+        for to, device in peers:
+            remote(
+                outs.at[kind, to], outr.at[kind, :, :, cols(q, bw)],
+                osem.at[kind], osem.at[2 + kind], device,
+            ).start()
+        outr[kind, :, :, cols(q, bw)] = outs[kind, q]
+
     def tick(t, carry):
         u = t - behind
         d = t - down_behind
@@ -537,6 +553,10 @@
         @pl.when(jnp.logical_and(s == last, jnp.logical_and(d >= 1, d < micro + 1)))
         def _():
             out_scale_grad(d - 1)
+
+        @pl.when(d == micro)
+        def _():
+            send_rows(0, ob)
 
         @pl.when(jnp.logical_and(u >= 2, u < micro + 2))
         def _():
@@ -561,31 +581,29 @@
         gtl[2 * members : 2 * members + 1, :] = jnp.sum(tables * in_tab[:, my_cols], axis=0, keepdims=True)
         gtab[:, my_cols] = gtl[...]
         for _, device in peers:
-            remote(gtl, gtab.at[:, my_cols], osem.at[0], osem.at[1], device).start()
-
-        for kind, src in ((0, ob), (1, ig)):
-            for k in range(micro):
-                rowf[...] = src[k].astype(F32)
-                for n in range(chips):
-                    for c in range(2):
-                        at = (n * 2 + c) * rows
-                        outs[n, (c * 2 + kind) * micro + k] = rowf[at : at + rows, :].astype(BF16)
-        for to, device in peers:
-            remote(outs.at[to], outr.at[:, :, cols(q, bw)], osem.at[2], osem.at[3], device).start()
-        outr[:, :, cols(q, bw)] = outs[q]
+            remote(gtl, gtab.at[:, my_cols], osem.at[4], osem.at[5], device).start()
+        send_rows(1, ig)
 
     with jax.named_scope("end_wait"):
         most = gtab.at[:, pl.ds(0, (chips - 1) * bw)]
-        remote(most, most, osem.at[0], osem.at[1], partner).wait_recv()
+        most_outs = [outs.at[kind, pl.ds(0, chips - 1)] for kind in range(2)]
+        rows_on = [
+            remote(
+                outr.at[kind, pl.ds(other * micro, micro)], outp.at[kind],
+                osem.at[6 + kind], osem.at[8 + kind], partner,
+            )
+            for kind in range(2)
+        ]
+        remote(most_outs[0], most_outs[0], osem.at[0], osem.at[2], partner).wait_recv()
+        rows_on[0].start()
+        remote(most, most, osem.at[4], osem.at[5], partner).wait_recv()
         table_part = gtab.at[:, core_cols]
-        tables_on = remote(table_part, table_part, osem.at[4], osem.at[5], partner)
+        tables_on = remote(table_part, table_part, osem.at[10], osem.at[11], partner)
         tables_on.start()
-        most_outs = outs.at[pl.ds(0, chips - 1)]
-        remote(most_outs, most_outs, osem.at[2], osem.at[3], partner).wait_recv()
-        rows_on = remote(outr.at[pl.ds(other * 2 * micro, 2 * micro)], outp, osem.at[6], osem.at[7], partner)
-        rows_on.start()
-        out_x[:, :, core_cols] = outr[pl.ds(core * 2 * micro, micro)]
-        out_g[:, :, core_cols] = outr[pl.ds((core * 2 + 1) * micro, micro)]
+        remote(most_outs[1], most_outs[1], osem.at[1], osem.at[3], partner).wait_recv()
+        rows_on[1].start()
+        out_x[:, :, core_cols] = outr[0, pl.ds(core * micro, micro)]
+        out_g[:, :, core_cols] = outr[1, pl.ds(core * micro, micro)]
 
     with jax.named_scope("end_sent"):
         for k in range(micro):
@@ -628,16 +646,18 @@
             first.wait_send()
             second.wait_send()
 
-        remote(most, most, osem.at[0], osem.at[1], partner).wait_send()
-        remote(most_outs, most_outs, osem.at[2], osem.at[3], partner).wait_send()
+        remote(most, most, osem.at[4], osem.at[5], partner).wait_send()
+        for kind in range(2):
+            remote(most_outs[kind], most_outs[kind], osem.at[kind], osem.at[2 + kind], partner).wait_send()
     with jax.named_scope("end_out"):
         tables_on.wait()
         g_in[...] = gtab[0:members, :]
         g_out[...] = gtab[members : 2 * members, :]
         g_gain[...] = gtab[2 * members : 2 * members + 1, :]
-        rows_on.wait()
-        out_x[:, :, cols(other, half)] = outp[0:micro]
-        out_g[:, :, cols(other, half)] = outp[micro : 2 * micro]
+        rows_on[0].wait()
+        out_x[:, :, cols(other, half)] = outp[0]
+        rows_on[1].wait()
+        out_g[:, :, cols(other, half)] = outp[1]
 
 
 def deliver(count, *refs):
@@ -701,7 +721,8 @@
             buf(micro, total, width, dtype=F32), buf(micro, total, width, dtype=F32),
             buf(all_tokens, hidden), buf(all_tokens, hidden), buf(all_tokens, hidden),
             buf(all_tokens, width), buf(all_tokens, width), buf(hidden, all_tokens),
-            buf(hidden, width), buf(hidden, width), buf(hidden, width),
+            buf(total, hidden, dtype=F32), buf(total, hidden, dtype=F32), buf(total, hidden, dtype=F32),
+            buf(2 * hidden, width), buf(hidden, width),
             buf(2 * chips, micro, rows, width),
             buf(2 * micro, rows, half),
             buf(chips, 2 * micro, rows, bw),
@@ -717,22 +738,22 @@
             buf(2, micro, chips, total, bw),
             buf(chips, total, bw, dtype=F32),
             buf(2, micro, chips, total, bw),
-            buf(micro, 8, total, dtype=F32), buf(micro, 8, total, dtype=F32),
-            buf(micro, 8, total, dtype=F32), buf(micro, chips, 8, total, dtype=F32),
+            buf(micro, 1, total, dtype=F32), buf(micro, 1, total, dtype=F32),
+            buf(micro, 1, total, dtype=F32), buf(micro, chips, 1, total, dtype=F32),
             buf(micro, total, bw, dtype=F32),
             buf(micro, total, bw), buf(micro, total, bw),
             buf(members, bw, dtype=F32), buf(members, bw, dtype=F32),
             buf(16, bw, dtype=F32), buf(16, width, dtype=F32),
-            buf(chips, 4 * micro, rows, bw),
-            buf(4 * micro, rows, half),
-            buf(2 * micro, rows, half),
+            buf(2, chips, 2 * micro, rows, bw),
+            buf(2, 2 * micro, rows, half),
+            buf(2, micro, rows, half),
             dma((7,)), dma((3,)), dma((4,)),
             dma((micro,)), dma((micro,)), dma((micro,)), dma((micro,)),
             dma((2, micro)), dma((2, micro)), dma((2, micro)), dma((2, micro)),
             dma((2, micro)), dma((2, micro)), dma((2, micro, 2)), dma((2, micro, 2)),
             dma((2, micro)), dma((2, micro)),
             dma((micro,)), dma((micro,)), dma((micro,)), dma((micro,)),
-            dma((8,)),
+            dma((12,)),
         ],
         compiler_params=pltpu.CompilerParams(
             collective_id=0, has_side_effects=True, vmem_limit_bytes=46 * 1024 * 1024

time: 174 us -> 171 us (0.983)
  Pallas kernels: 173 us -> 170 us
    pallas_call x1, Pallas kernels: 169 us -> 165 us  [on_device(): pl.pallas_call(functools.partial(relay_kernel, dims), name='relay', out_s...]
where the time goes in v4:
time: 171 us
  Pallas kernels  170 us (99%)
    pallas_call x1, Pallas kernels, on_device(): pl.pallas_call(functools.partial(relay_kernel, dims), name='relay', out_s...  165 us
    pallas_call x1, Pallas kernels, on_device(): pl.pallas_call(functools.partial(deliver, len(outs)), name='deliver', out...  4.38 us

profile of v4, /device:TPU:1, one launch (start us, length us, event | category | flops | bytes accessed | tf_op | source)
XLA Modules:
  0.0 170.5 jit_solution(10375826037736644930)
XLA Ops:
  0.6 165.3 %relay.1 = (bf16[3,2,4096]{2,1,0:T(2,128)(2,1)S(1)}, bf16[3,2,4096]{2,1,0:T(2,128)(2,1)S(1)}, bf16[448,4096]{1,0:T(8,128)(2,1)S(1)}, bf16[448,4096]{1,0:T(8,128)...) custom-call(bf16[3,2,4096]{2,1,0:T(2,128)(2,1)} %tok_h.1, ...), custom_call_target="tpu_custom_call" | custom-call | tf_op jit(solution)/shard_map/relay/pallas_call | solution.py:711
  166.0 4.4 %deliver.1 = (bf16[3,2,4096]{2,1,0:T(2,128)(2,1)}, bf16[3,2,4096]{2,1,0:T(2,128)(2,1)}, bf16[448,4096]{1,0:T(8,128)(2,1)}, bf16[448,4096]{1,0:T(8,128)(2,1)}, bf...) custom-call(bf16[3,2,4096]{2,1,0:T(2,128)(2,1)S(1)} %get-tuple-eleme, ...), custom_call_target="tpu_custom_call" | custom-call | tf_op jit(solution)/shard_map/deliver/pallas_call | solution.py:766

commit v5 on v4

--- a/solution.py
+++ b/solution.py
@@ -68,7 +68,11 @@
     def ups(d):
         return (d[0] if d[0] * 2 <= across else 0) + (d[1] if d[1] <= mps else 0)
 
-    offsets.sort(key=lambda d: (-ups(d), -hops(d)))
+    def downs(d):
+        x, y = (across - d[0]) % across, (2 * mps - d[1]) % (2 * mps)
+        return (x if x * 2 <= across else 0) + (y if y <= mps else 0)
+
+    offsets.sort(key=lambda d: (-downs(d), -hops(d)))
     reach = max(map(hops, offsets)) // 2
 
     def chip(dx, dy):

time: 171 us -> 171 us (level)
  no operation moved by 1% of the time
where the time goes in v5:
time: 171 us
  Pallas kernels  170 us (99%)
    pallas_call x1, Pallas kernels, on_device(): pl.pallas_call(functools.partial(relay_kernel, dims), name='relay', out_s...  165 us
    pallas_call x1, Pallas kernels, on_device(): pl.pallas_call(functools.partial(deliver, len(outs)), name='deliver', out...  4.38 us

profile of v5, /device:TPU:1, one launch (start us, length us, event | category | flops | bytes accessed | tf_op | source)
XLA Modules:
  0.0 170.6 jit_solution(11851123211953957549)
XLA Ops:
  0.6 165.5 %relay.1 = (bf16[3,2,4096]{2,1,0:T(2,128)(2,1)S(1)}, bf16[3,2,4096]{2,1,0:T(2,128)(2,1)S(1)}, bf16[448,4096]{1,0:T(8,128)(2,1)S(1)}, bf16[448,4096]{1,0:T(8,128)...) custom-call(bf16[3,2,4096]{2,1,0:T(2,128)(2,1)} %tok_h.1, ...), custom_call_target="tpu_custom_call" | custom-call | tf_op jit(solution)/shard_map/relay/pallas_call | solution.py:715
  166.1 4.4 %deliver.1 = (bf16[3,2,4096]{2,1,0:T(2,128)(2,1)}, bf16[3,2,4096]{2,1,0:T(2,128)(2,1)}, bf16[448,4096]{1,0:T(8,128)(2,1)}, bf16[448,4096]{1,0:T(8,128)(2,1)}, bf...) custom-call(bf16[3,2,4096]{2,1,0:T(2,128)(2,1)S(1)} %get-tuple-eleme, ...), custom_call_target="tpu_custom_call" | custom-call | tf_op jit(solution)/shard_map/deliver/pallas_call | solution.py:770
